TPU v7x, 32 devices: a whole 2x2x4 slice. The times are simulated.
32 devices in a mesh: groups: 2 (over y), expert: 4 (over z), dp: 2 (over core), tensor: 2 (over x).
Axes of the slice: x: 2, y: 2, z: 4, core: 2. Of those that a mesh axis runs over, the one named last changes fastest.
Arguments:
- tokens: bfloat16 [2, 2048, 2048], P('dp', ('groups', 'expert', 'tensor')), parts along dimension 1, may hold values from -6 to 6
- proj_weight: bfloat16 [4, 2048, 3584], P('expert', 'dp', 'tensor'), may hold values from -0.125 to 0.125
- slot_grads: bfloat16 [2, 4, 32, 3584], P('dp', 'expert', 'groups', 'tensor'), parts along dimension 2, may hold values from -1.5 to 1.5
- gate_weights: float32 [2, 2, 32], P('dp', None, 'groups'), parts along dimension 2, may hold values from 0.2 to 1
- selected: int32 [2, 2, 32], P('dp', None, 'groups'), parts along dimension 2, may hold values from 0 to 1023, as said below
Outputs:
- token_grads: bfloat16 [2, 2048, 2048], P('dp', ('groups', 'expert', 'tensor')), parts along dimension 1
- weight_grads: bfloat16 [8, 2048, 3584], P(('groups', 'expert'), 'dp', 'tensor'), parts along dimension 0
There are 2 independent parts, one for each index of `groups`. A program takes and returns all parts, laid end to end along the dimension named above; an argument that names none is the same for every part. Nothing has to cross between parts.
Inputs may be any that keep to these rules, and one draw needn't show every extreme that they name: `selected`: each entry names a token of its own group. Within one group and one expert the 16 entries are distinct. In each group an expert takes at most 4 tokens from the 128 tokens of one device (tokens k * 128 to (k + 1) * 128 - 1), and exactly 4 from some devices.
All inputs are finite; a program needn't handle non-finite values.
Results may differ from a plain program's by a relative error of at most 0.011.
Values may be sent and summed in bfloat16 or wider, within the bound.
No kernel may reach another device: no remote copies, remote signals or barrier semaphores. Data moves between devices by JAX's collectives and lax.ppermute only.
A program may use at most 64 MiB of HBM per device.

v0:
```python
import jax
import jax.numpy as jnp
from jax import lax
from jax.sharding import PartitionSpec as P

MOST = 4


def local(tokens, proj_weight, slot_grads, gate_weights, selected):
    n_tensor = lax.axis_size("tensor")
    n_expert = lax.axis_size("expert")
    n_data = lax.axis_size("dp")
    owners = n_expert * n_tensor
    own_expert = lax.axis_index("expert")
    own_owner = own_expert * n_tensor + lax.axis_index("tensor")
    token_rows = tokens[0]
    tok_dev = token_rows.shape[0]
    features = token_rows.shape[1]
    chosen = selected[0]
    experts = chosen.shape[0]
    capacity = chosen.shape[1]
    owner_of = chosen // tok_dev
    local_row = chosen % tok_dev
    slot_ids = jnp.arange(capacity)
    earlier = slot_ids[None, :] < slot_ids[:, None]
    same_owner = owner_of[:, :, None] == owner_of[:, None, :]
    arrival = jnp.sum(same_owner & earlier[None], axis=2)
    slot_pos = jnp.arange(MOST)
    local_hits = owner_of == own_owner
    selector = local_hits[:, None, :] & (arrival[:, None, :] == slot_pos[None, :, None])
    filled = jnp.any(selector, axis=2)
    send_row = jnp.sum(jnp.where(selector, local_row[:, None, :], 0), axis=2)
    outgoing = jnp.where(filled[..., None], token_rows[send_row], jnp.zeros((), jnp.bfloat16))
    outgoing_all = jnp.broadcast_to(outgoing[:, None, None], (experts, 2, n_tensor, MOST, features))
    incoming = lax.all_to_all(
        outgoing_all.reshape(owners, MOST, features),
        ("expert", "tensor"),
        split_axis=0,
        concat_axis=0,
        tiled=True,
    )
    incoming = incoming.reshape(owners * MOST, features)
    own_index = own_expert // 2
    own_owners = lax.dynamic_index_in_dim(owner_of, own_index, 0, keepdims=False)
    own_arrival = lax.dynamic_index_in_dim(arrival, own_index, 0, keepdims=False)
    slot_rows = incoming[own_owners * MOST + own_arrival]
    gate_row = lax.dynamic_index_in_dim(gate_weights[0], own_index, 0, keepdims=False)
    scaled = (gate_row[:, None] * slot_grads[0, 0].astype(jnp.float32)).astype(jnp.bfloat16)
    partial_value_sum = lax.dot_general(
        scaled,
        lax.all_gather(proj_weight, "dp", axis=1, tiled=True)[0],
        (((1,), (1,)), ((), ())),
        preferred_element_type=jnp.float32,
    ).astype(jnp.bfloat16)
    slot_equal_mask = (own_owners[None, None, :] == jnp.arange(owners)[:, None, None]) & (
        own_arrival[None, None, :] == slot_pos[None, :, None]
    )
    slot_used = jnp.any(slot_equal_mask, axis=2)
    slot_index = jnp.sum(jnp.where(slot_equal_mask, slot_ids[None, None, :], 0), axis=2)
    returning = jnp.where(
        slot_used[..., None], partial_value_sum[slot_index], jnp.zeros((), jnp.bfloat16)
    )
    arrived = lax.all_to_all(
        returning, ("expert", "tensor"), split_axis=0, concat_axis=0, tiled=True
    )
    arrived = arrived.reshape(owners * MOST, features)
    complete_row = jnp.broadcast_to(send_row[:, None, None], (experts, 2, n_tensor, MOST)).reshape(
        owners * MOST
    )
    used_full = jnp.broadcast_to(filled[:, None, None], (experts, 2, n_tensor, MOST)).reshape(
        owners * MOST
    )
    placement = (jnp.arange(tok_dev)[:, None] == complete_row[None, :]) & used_full[None, :]
    token_grads = jnp.dot(
        placement.astype(jnp.bfloat16), arrived, preferred_element_type=jnp.float32
    )
    token_grads = token_grads.astype(jnp.bfloat16)[None]
    column_share = lax.all_to_all(slot_rows, "dp", split_axis=1, concat_axis=0, tiled=True)
    scaled_all = lax.all_gather(scaled, "dp", axis=0, tiled=True)
    column_share = column_share.reshape(n_data, capacity, column_share.shape[1])
    scaled_all = scaled_all.reshape(n_data, capacity, scaled_all.shape[1])
    per_group = jnp.einsum(
        "gcd,gcf->gdf", column_share, scaled_all, preferred_element_type=jnp.float32
    )
    per_group = per_group.astype(jnp.bfloat16).astype(jnp.float32)
    weight_grads = jnp.sum(per_group, axis=0).astype(jnp.bfloat16)[None]
    return (token_grads, weight_grads)


def solution(mesh):
    in_specs = (
        P("dp", ("groups", "expert", "tensor"), None),
        P("expert", "dp", "tensor"),
        P("dp", "expert", "groups", "tensor"),
        P("dp", None, "groups"),
        P("dp", None, "groups"),
    )
    out_specs = (
        P("dp", ("groups", "expert", "tensor"), None),
        P(("groups", "expert"), "dp", "tensor"),
    )
    return jax.shard_map(local, mesh=mesh, in_specs=in_specs, out_specs=out_specs, check_vma=False)
```

profile of v0, /device:TPU:0, one launch (start us, length us, event | category | flops | bytes accessed | tf_op | source)
XLA Modules:
  0.0 58.4 jit_solution(3440165395489555670)
XLA Ops:
  7.2 0.7 %all-gather.2.cloned.1.call-update = ((bf16[1,1024,1792]{2,1,0:T(8,128)(2,1)}), bf16[1,2048,1792]{2,1,0:T(8,128)(2,1)}) async-update(((), (), s32[]{:S(2)}) %all-gather.2.cloned.1.call-start, bf16[1,1024,1792]{2,1,0:T(8,128)(2,1)} %param.6) | async-update | bytes 14680088
  7.9 0.7 %broadcast_compare_fusion = (pred[2,16]{1,0:T(4,128)(4,1)S(1)}, s32[2,16]{1,0:T(2,128)S(1)}) fusion(s32[]{:T(128)S(6)} %add.79, s32[1,2,16]{2,1,0:T(2,128)} %param.9), kind=kLoop, calls=%fused_computation.53 | loop fusion | flops 512 | bytes 292 | tf_op jit(solution)/shard_map/eq | solution.py:29
  8.6 0.2 convert_reduce_fusion.1
  8.8 0.7 %and_select_fusion.1 = s32[2,16]{1,0:T(2,128)S(1)} fusion(s32[1,2,16]{2,1,0:T(2,128)} %param.9), kind=kLoop, calls=%fused_computation.41 | loop fusion | flops 352 | bytes 256 | tf_op jit(solution)/shard_map/jit(remainder)/select_n | solution.py:23
  9.8 0.6 gather_fusion.1
  10.4 0.2 fusion.19
  10.6 0.7 %broadcast_in_dim.104 = bf16[2,2,2,4,2048]{4,3,2,1,0:T(4,128)(2,1)} broadcast(bf16[2,4,2048]{2,1,0:T(4,128)(2,1)S(1)} %broadcast_select_fusion.1), dimensions={0,3,4} | broadcast | bytes 163840 | tf_op jit(solution)/shard_map/broadcast_in_dim | solution.py:34
  11.3 7.3 %all-to-all-start.1 = ((bf16[8,4,2048]{2,1,0:T(4,128)(2,1)}), bf16[8,4,2048]{2,1,0:T(4,128)(2,1)S(1)}, u32[]{:S(2)}, u32[]{:S(2)}) async-start(bf16[8,4,2048]{2,1,0:T(4,128)(2,1)} %bitcast.10), calls=%async_computation.1 | async-start | bytes 262144 | tf_op jit(solution)/shard_map/all_to_all | solution.py:35
  18.6 0.7 %fusion.20 = f32[16]{0:T(128)S(1)} fusion(f32[1,2,16]{2,1,0:T(2,128)} %param.8, s32[]{:T(128)S(6)} %select_n.92), kind=kLoop, calls=%fused_computation.51 | loop fusion | bytes 132 | tf_op jit(solution)/shard_map/jit(dynamic_index_in_dim)/dynamic_slice | solution.py:47
  19.3 0.2 and_reduce_fusion
  19.5 0.2 fusion.17
  19.6 0.9 %fusion.8 = bf16[16,1792]{1,0:T(8,128)(2,1)S(1)} fusion(bf16[1,1,16,1792]{3,2,1,0:T(8,128)(2,1)} %param.7, f32[16]{0:T(128)S(1)} %fusion.20), kind=kLoop, calls=%fused_computation.14 | loop fusion | flops 86016 | bytes 114752 | tf_op jit(solution)/shard_map/convert_element_type | solution.py:48
  21.0 4.9 %all-to-all-done.1 = bf16[8,4,2048]{2,1,0:T(4,128)(2,1)S(1)} async-done(((bf16[8,4,2048]{2,1,0:T(4,128)(2,1)}), bf16[8,4,2048]{2,1,0:T(4,128)(2,1)S(1)}, u32[]{:S(2)}, u32[]{:S(2)}) %all-to-all-start.1) | async-done | bytes 131104 | tf_op jit(solution)/shard_map/all_to_all | solution.py:35
  26.0 0.6 %gather_fusion.2 = bf16[16,2048]{1,0:T(8,128)(2,1)S(1)} fusion(bf16[32,2048]{1,0:T(8,128)(2,1)S(1)} %reshape.252, s32[1024]{0:T(1024)S(1)} %pad_clamp_fusion), kind=kCustom, calls=%fused_computation.2 | custom fusion | bytes 131136 | tf_op jit(solution)/shard_map/gather | solution.py:46
  26.6 0.6 %copy.15 = bf16[2,2,8,1024]{3,2,0,1:T(8,128)(2,1)} copy(bf16[2,2,8,1024]{3,2,1,0:T(8,128)(2,1)S(1)} %bitcast.71) | data formatting | bytes 131072 | tf_op jit(solution)/shard_map/all_to_all | solution.py:78
  27.2 3.3 %all-to-all-start.2 = ((bf16[16,2,1024]{2,0,1:T(8,128)(2,1)}), bf16[16,2,1024]{2,0,1:T(8,128)(2,1)S(1)}, u32[]{:S(2)}, u32[]{:S(2)}) async-start(bf16[16,2,1024]{2,0,1:T(8,128)(2,1)} %bitcast.67), calls=%async_computation.2 | async-start | bytes 131072 | tf_op jit(solution)/shard_map/all_to_all | solution.py:78
  30.6 5.1 %fusion.3 = bf16[16,2048]{1,0:T(8,128)(2,1)S(1)} fusion(bf16[1,2048,1792]{2,1,0:T(8,128)(2,1)} %all-gather.2.cloned.1.call-done, bf16[1,1,16,1792]{3,2,1,0:T(8,128)(2,1)} %param.7, f32[16]{0:T(128)S(1)} %fusion.20), kind=kOutput, calls=%fused_computation.8 | convolution fusion | flops 117559296 | bytes 7462976 | tf_op jit(solution)/shard_map/dot_general | solution.py:49
  35.7 0.7 %gather_fusion = bf16[32,2048]{1,0:T(8,128)(2,1)S(1)} fusion(bf16[16,2048]{1,0:T(8,128)(2,1)S(1)} %fusion.3, s32[1024]{0:T(1024)S(1)} %pad_clamp_fusion.2), kind=kCustom, calls=%fused_computation | custom fusion | bytes 262272 | tf_op jit(solution)/shard_map/gather | solution.py:61
  36.4 0.8 %broadcast_select_fusion = bf16[8,4,2048]{2,1,0:T(4,128)(2,1)} fusion(bf16[8,4,2048]{2,1,0:T(4,128)(2,1)S(1)} %reshape.256, pred[8,4]{1,0:T(8,128)(4,1)S(1)} %copy.10), kind=kLoop, calls=%fused_computation.11 | loop fusion | flops 65536 | bytes 262176 | tf_op jit(solution)/shard_map/jit(_where)/select_n | solution.py:60
  37.2 5.8 %all-to-all-start = ((bf16[8,4,2048]{2,1,0:T(4,128)(2,1)}), bf16[8,4,2048]{2,1,0:T(4,128)(2,1)S(1)}, u32[]{:S(2)}, u32[]{:S(2)}) async-start(bf16[8,4,2048]{2,1,0:T(4,128)(2,1)} %broadcast_select_fusion), calls=%async_computation | async-start | bytes 262144 | tf_op jit(solution)/shard_map/all_to_all | solution.py:63
  43.0 1.9 %all_gather.7 = bf16[32,1792]{1,0:T(8,128)(2,1)S(1)} all-gather(bf16[16,1792]{1,0:T(8,128)(2,1)S(1)} %fusion.8), channel_id=1, replica_groups=mesh['groups'=2,'expert'=4,'dp'=2,'tensor'=2] {'dp'}, dimensions={0}, use_global_device_ids=true | all-gather | bytes 172032 | tf_op jit(solution)/shard_map/all_gather | solution.py:79
  44.9 4.3 %convert_reduce_fusion = bf16[1024,1792]{1,0:T(8,128)(2,1)} fusion(bf16[2,16,1792]{2,1,0:T(8,128)(2,1)S(1)} %bitcast.70, bf16[16,2,1024]{2,0,1:T(8,128)(2,1)S(1)} %all-to-all-done.2), kind=kOutput, calls=%fused_computation.5 | convolution fusion | flops 122945536 | bytes 3850240 | tf_op jit(solution)/shard_map/gcd,gcf->gdf/dot_general | solution.py:82
  49.2 1.3 %all-to-all-done = bf16[8,4,2048]{2,1,0:T(4,128)(2,1)S(1)} async-done(((bf16[8,4,2048]{2,1,0:T(4,128)(2,1)}), bf16[8,4,2048]{2,1,0:T(4,128)(2,1)S(1)}, u32[]{:S(2)}, u32[]{:S(2)}) %all-to-all-start) | async-done | bytes 131104 | tf_op jit(solution)/shard_map/all_to_all | solution.py:63
  50.5 1.1 %fusion.2 = bf16[1,128,2048]{2,1,0:T(8,128)(2,1)} fusion(bf16[32,2048]{1,0:T(8,128)(2,1)S(1)} %reshape.250, s32[32]{0:T(128)S(1)} %eq.100, pred[32]{0:T(512)(128)(4,1)S(1)} %and.91), kind=kOutput, calls=%fused_computation.7 | convolution fusion | flops 17047552 | bytes 655520 | tf_op jit(solution)/shard_map/dot_general | solution.py:74
  (29 shorter events, 1.1 us)
Async XLA Ops:
  7.2 2.6 %copy-start = (bf16[1,128,2048]{2,1,0:T(8,128)(2,1)S(1)}, bf16[1,128,2048]{2,1,0:T(8,128)(2,1)}, u32[]{:S(2)}) copy-start(bf16[1,128,2048]{2,1,0:T(8,128)(2,1)} %param.5) | copy-start | bytes 1572868
  7.2 23.4 %all-gather.2.cloned.1.call-start = ((), (), s32[]{:S(2)}) async-start(), calls=%async_computation.3 | async-start | bytes 11010048 | tf_op jit(solution)/shard_map/all_gather | solution.py:51
  11.3 14.6 %all-to-all-start.1 = ((bf16[8,4,2048]{2,1,0:T(4,128)(2,1)}), bf16[8,4,2048]{2,1,0:T(4,128)(2,1)S(1)}, u32[]{:S(2)}, u32[]{:S(2)}) async-start(bf16[8,4,2048]{2,1,0:T(4,128)(2,1)} %bitcast.10), calls=%async_computation.1 | async-start | bytes 262144 | tf_op jit(solution)/shard_map/all_to_all | solution.py:35
  27.2 10.0 %all-to-all-start.2 = ((bf16[16,2,1024]{2,0,1:T(8,128)(2,1)}), bf16[16,2,1024]{2,0,1:T(8,128)(2,1)S(1)}, u32[]{:S(2)}, u32[]{:S(2)}) async-start(bf16[16,2,1024]{2,0,1:T(8,128)(2,1)} %bitcast.67), calls=%async_computation.2 | async-start | bytes 131072 | tf_op jit(solution)/shard_map/all_to_all | solution.py:78
  37.2 13.3 %all-to-all-start = ((bf16[8,4,2048]{2,1,0:T(4,128)(2,1)}), bf16[8,4,2048]{2,1,0:T(4,128)(2,1)S(1)}, u32[]{:S(2)}, u32[]{:S(2)}) async-start(bf16[8,4,2048]{2,1,0:T(4,128)(2,1)} %broadcast_select_fusion), calls=%async_computation | async-start | bytes 262144 | tf_op jit(solution)/shard_map/all_to_all | solution.py:63
Sparse Core Ops, SparseCore 0:
  9.5 21.0 all-gather.1
where the time goes:
time: 59 us; the launch traced here: 58.4 us
  starting transfers between devices  16.4 us (28%)
  between operations  14.1 us (24%)
  matrix products  10.5 us (18%)
  waiting for transfers between devices  6.92 us (12%)
  local copies, waits for them, and re-layouts  4.56 us (8%)
  other arithmetic  4.02 us (7%)
  blocking collectives  1.88 us (3%)
    all_to_all x1, starting transfers between devices, local(): lax.all_to_all(outgoing_all.reshape(owners, MOST, features), ('expert', '...  7.28 us
    all_to_all x1, starting transfers between devices, local(): lax.all_to_all(returning, ('expert', 'tensor'), split_axis=0, concat_axis...  5.83 us
    dot_general x1, matrix products, local(): lax.dot_general(scaled, lax.all_gather(proj_weight, 'dp', axis=1, tiled=T...  5.11 us
    all_to_all x1, waiting for transfers between devices, local(): lax.all_to_all(outgoing_all.reshape(owners, MOST, features), ('expert', '...  4.91 us
    dot_general x1, matrix products, local(): jnp.einsum('gcd,gcf->gdf', column_share, scaled_all, preferred_element_ty...  4.31 us
    all_to_all x1, starting transfers between devices, local(): lax.all_to_all(slot_rows, 'dp', split_axis=1, concat_axis=0, tiled=True)  3.3 us
    all_gather x1, blocking collectives, local(): scaled_all = lax.all_gather(scaled, 'dp', axis=0, tiled=True)  1.88 us
    all_to_all x1, waiting for transfers between devices, local(): lax.all_to_all(returning, ('expert', 'tensor'), split_axis=0, concat_axis...  1.25 us
  transfers between devices with their start and end apart: 4, of which 3 were waited for; matrix products, arithmetic and copies ran while one was open for 31% of the time, Pallas kernels for 0%

commit v1 on v0

v1 whole, which is shorter than its diff:
```python
import functools

import jax
import jax.numpy as jnp
from jax import lax
from jax.experimental import pallas as pl
from jax.experimental.pallas import tpu as pltpu
from jax.sharding import PartitionSpec as P

MOST = 4
BF16 = jnp.bfloat16
F32 = jnp.float32
VMEM = pl.BlockSpec(memory_space=pltpu.VMEM)


def params(limit_mib=24):
    return pltpu.CompilerParams(vmem_limit_bytes=limit_mib * 2**20)


def to_column(row):
    n = row.shape[1]
    eye = lax.broadcasted_iota(jnp.int32, (n, n), 0) == lax.broadcasted_iota(jnp.int32, (n, n), 1)
    return jnp.sum(jnp.where(eye, row, jnp.zeros_like(row)), axis=1, keepdims=True)


def owner_and_arrival(chosen, tok_dev):
    n = chosen.shape[1]
    owner = chosen // tok_dev
    before = lax.broadcasted_iota(jnp.int32, (n, n), 0) < lax.broadcasted_iota(jnp.int32, (n, n), 1)
    same = to_column(owner) == owner
    arrival = jnp.sum(jnp.where(same & before, 1, 0), axis=0, keepdims=True)
    return owner, arrival


def own_rows(chosen_ref, owner_id, tok_dev):
    out = []
    for e in range(chosen_ref.shape[0]):
        chosen = chosen_ref[e : e + 1, :]
        owner, arrival = owner_and_arrival(chosen, tok_dev)
        place = jnp.where(owner == owner_id, arrival, -1)
        hit = lax.broadcasted_iota(jnp.int32, (MOST, chosen.shape[1]), 0) == place
        out.append(jnp.sum(jnp.where(hit, chosen - owner * tok_dev + 1, 0), axis=1, keepdims=True))
    return jnp.concatenate(out, axis=0)


def prep_kernel(n_expert, n_tensor, n_data, chosen_ref, gate_ref, grads_ref, tokens_ref, send_ref, scaled_ref):
    tok_dev, features = tokens_ref.shape
    experts = chosen_ref.shape[0]
    halves = n_expert // experts
    share = features // n_data
    own_half = lax.axis_index("expert")
    owner_id = own_half * n_tensor + lax.axis_index("tensor")
    target = own_rows(chosen_ref, owner_id, tok_dev)
    onehot = (lax.broadcasted_iota(jnp.int32, (experts * MOST, tok_dev), 1) + 1 == target).astype(F32).astype(BF16)
    rows = jnp.dot(onehot, tokens_ref[...], preferred_element_type=F32)
    for e in range(experts):
        block = rows[e * MOST : (e + 1) * MOST].astype(BF16)
        for d in range(n_data):
            piece = block[:, d * share : (d + 1) * share]
            for k in range(halves * n_tensor):
                send_ref[(d * experts + e) * halves * n_tensor + k] = piece
    own_expert = own_half // halves
    chosen = chosen_ref[pl.ds(own_expert, 1), :]
    owner, arrival = owner_and_arrival(chosen, tok_dev)
    places = n_expert * n_tensor * MOST
    capacity = chosen.shape[1]
    spread = lax.broadcasted_iota(jnp.int32, (places, capacity), 0) == owner * MOST + arrival
    gate = to_column(gate_ref[pl.ds(own_expert, 1), :])
    scaled = (gate * grads_ref[...].astype(F32)).astype(BF16)
    scaled_ref[...] = jnp.dot(spread.astype(F32).astype(BF16), scaled, preferred_element_type=F32).astype(BF16)


def partial_kernel(own_ref, other_ref, weight_ref, part_ref, all_ref):
    places = own_ref.shape[0]
    group = lax.axis_index("dp")
    all_ref[pl.ds(pl.multiple_of(group * places, places), places), :] = own_ref[...]
    all_ref[pl.ds(pl.multiple_of((1 - group) * places, places), places), :] = other_ref[...]
    part = lax.dot_general(
        all_ref[...], weight_ref[...], (((1,), (1,)), ((), ())), preferred_element_type=F32
    )
    part_ref[...] = part.astype(BF16)


def weight_kernel(rows_ref, scaled_ref, out_ref):
    out_ref[...] = lax.dot_general(
        rows_ref[...], scaled_ref[...], (((0,), (0,)), ((), ())), preferred_element_type=F32
    ).astype(BF16)


def token_kernel(n_expert, n_tensor, n_data, chosen_ref, parts_ref, out_ref):
    tok_dev, features = out_ref.shape
    experts = chosen_ref.shape[0]
    halves = n_expert // experts
    share = features // n_data
    owner_id = lax.axis_index("expert") * n_tensor + lax.axis_index("tensor")
    target = own_rows(chosen_ref, owner_id, tok_dev)
    wide = jnp.concatenate(
        [target[e * MOST : (e + 1) * MOST] for e in range(experts) for _ in range(halves * n_tensor)], axis=0
    )
    places = wide.shape[0]
    onehot = (lax.broadcasted_iota(jnp.int32, (places, tok_dev), 1) + 1 == wide).astype(F32).astype(BF16)
    for d in range(n_data):
        out_ref[:, d * share : (d + 1) * share] = lax.dot_general(
            onehot,
            parts_ref[d * places : (d + 1) * places, :],
            (((0,), (0,)), ((), ())),
            preferred_element_type=F32,
        ).astype(BF16)


def exchange(blocks):
    return lax.all_to_all(blocks, ("dp", "expert", "tensor"), split_axis=0, concat_axis=0, tiled=True)


def local(tokens, proj_weight, slot_grads, gate_weights, selected):
    n_tensor = lax.axis_size("tensor")
    n_expert = lax.axis_size("expert")
    n_data = lax.axis_size("dp")
    sizes = (n_expert, n_tensor, n_data)
    members = n_expert * n_tensor * n_data
    places = n_expert * n_tensor * MOST
    tok_dev, features = tokens.shape[1:]
    hidden = proj_weight.shape[2]
    share = features // n_data
    send, own = pl.pallas_call(
        functools.partial(prep_kernel, *sizes),
        out_shape=(
            jax.ShapeDtypeStruct((members, MOST, share), BF16),
            jax.ShapeDtypeStruct((places, hidden), BF16),
        ),
        in_specs=[VMEM] * 4,
        out_specs=(VMEM, VMEM),
        compiler_params=params(),
        cost_estimate=pl.CostEstimate(flops=10**8, bytes_accessed=10**6, transcendentals=0),
        name="prep",
    )(selected[0], gate_weights[0], slot_grads[0, 0], tokens[0])
    other = lax.ppermute(own, "dp", [(0, 1), (1, 0)])
    arrived = exchange(send)
    part, scaled = pl.pallas_call(
        partial_kernel,
        out_shape=(
            jax.ShapeDtypeStruct((n_data * places, share), BF16),
            jax.ShapeDtypeStruct((n_data * places, hidden), BF16),
        ),
        in_specs=[VMEM] * 3,
        out_specs=(VMEM, VMEM),
        compiler_params=params(),
        cost_estimate=pl.CostEstimate(flops=10**9, bytes_accessed=4 * 10**6, transcendentals=0),
        name="partial",
    )(own, other, proj_weight[0])
    returned = exchange(part.reshape(members, MOST, share))
    rows = arrived.reshape(n_data * places, share)
    block = min(256, share)
    weight_grads = pl.pallas_call(
        weight_kernel,
        grid=(share // block,),
        out_shape=jax.ShapeDtypeStruct((share, hidden), BF16),
        in_specs=[
            pl.BlockSpec((n_data * places, block), lambda i: (0, i)),
            pl.BlockSpec((n_data * places, hidden), lambda i: (0, 0)),
        ],
        out_specs=pl.BlockSpec((block, hidden), lambda i: (i, 0)),
        compiler_params=params(),
        cost_estimate=pl.CostEstimate(flops=10**9, bytes_accessed=4 * 10**6, transcendentals=0),
        name="weight_grad",
    )(rows, scaled)
    token_grads = pl.pallas_call(
        functools.partial(token_kernel, *sizes),
        out_shape=jax.ShapeDtypeStruct((tok_dev, features), BF16),
        in_specs=[VMEM] * 2,
        out_specs=VMEM,
        compiler_params=params(),
        cost_estimate=pl.CostEstimate(flops=10**8, bytes_accessed=10**6, transcendentals=0),
        name="token_grad",
    )(selected[0], returned.reshape(n_data * places, share))
    return token_grads[None], weight_grads[None]


def solution(mesh):
    in_specs = (
        P("dp", ("groups", "expert", "tensor"), None),
        P("expert", "dp", "tensor"),
        P("dp", "expert", "groups", "tensor"),
        P("dp", None, "groups"),
        P("dp", None, "groups"),
    )
    out_specs = (
        P("dp", ("groups", "expert", "tensor"), None),
        P(("groups", "expert"), "dp", "tensor"),
    )
    return jax.shard_map(local, mesh=mesh, in_specs=in_specs, out_specs=out_specs, check_vma=False)
```

time: 59 us -> 33.2 us (0.56)
  between operations: 14.1 us -> 0.68 us
  matrix products: 10.5 us -> 0 us
  Pallas kernels: 0 us -> 6.86 us
  starting transfers between devices: 16.4 us -> 11.5 us
  other arithmetic: 4.02 us -> 0 us
  blocking collectives: 1.88 us -> 0 us
  local copies, waits for them, and re-layouts: 4.56 us -> 6.03 us
  waiting for transfers between devices: 6.92 us -> 7.67 us
    dot_general x3 -> x0, matrix products: 10.5 us -> none  [the longest x1 5.11 us: local(): lax.dot_general(scaled, lax.all_gather(proj_weight, 'dp', axis=1, tiled=T...]
    pallas_call x0 -> x4, Pallas kernels: none -> 6.86 us  [the longest x1 3.18 us: local(): pl.pallas_call(weight_kernel, grid=(share // block,), out_shape=jax.Shape...]
    all_to_all x3 -> x2, starting transfers between devices: 16.4 us -> 11.1 us  [exchange(): lax.all_to_all(blocks, ('dp', 'expert', 'tensor'), split_axis=0, concat_a...]
    unnamed x2 -> x12, local copies, waits for them, and re-layouts: 0.01 us -> 5.25 us
    gather x5 -> x0, local copies, waits for them, and re-layouts: 1.93 us -> none  [the longest x2 0.73 us: local(): partial_value_sum[slot_index]]
    all_gather x1 -> x0, blocking collectives: 1.88 us -> none  [local(): scaled_all = lax.all_gather(scaled, 'dp', axis=0, tiled=True)]
    select_n x6 -> x0, other arithmetic: 1.58 us -> none  [the longest x1 0.78 us: local(): jnp.where(slot_used[..., None], partial_value_sum[slot_index], jnp.zeros(...]
    ppermute x0 -> x1, waiting for transfers between devices: none -> 1.03 us  [local(): other = lax.ppermute(own, 'dp', [(0, 1), (1, 0)])]
  transfers between devices with their start and end apart: 4 -> 3, of which waited for: 3 -> 3; matrix products, arithmetic and copies ran while one was open for 31% -> 2% of each run, Pallas kernels for 0% -> 13%
where the time goes in v1:
time: 33.2 us; the launch traced here: 32.7 us
  starting transfers between devices  11.5 us (35%)
  waiting for transfers between devices  7.67 us (23%)
  Pallas kernels  6.86 us (21%)
  local copies, waits for them, and re-layouts  6.03 us (18%)
  between operations  0.68 us (2%)
    all_to_all x2, starting transfers between devices, exchange(): lax.all_to_all(blocks, ('dp', 'expert', 'tensor'), split_axis=0, concat_a...  11.1 us
    all_to_all x2, waiting for transfers between devices, exchange(): lax.all_to_all(blocks, ('dp', 'expert', 'tensor'), split_axis=0, concat_a...  6.64 us
    unnamed x12, local copies, waits for them, and re-layouts  5.25 us
    pallas_call x1, Pallas kernels, local(): pl.pallas_call(weight_kernel, grid=(share // block,), out_shape=jax.Shape...  3.18 us
    pallas_call x1, Pallas kernels, local(): pl.pallas_call(functools.partial(token_kernel, *sizes), out_shape=jax.Sha...  1.38 us
    pallas_call x1, Pallas kernels, local(): pl.pallas_call(partial_kernel, out_shape=(jax.ShapeDtypeStruct((n_data *...  1.21 us
    pallas_call x1, Pallas kernels, local(): pl.pallas_call(functools.partial(prep_kernel, *sizes), out_shape=(jax.Sha...  1.09 us
    ppermute x1, waiting for transfers between devices, local(): other = lax.ppermute(own, 'dp', [(0, 1), (1, 0)])  1.03 us
  transfers between devices with their start and end apart: 3, of which 3 were waited for; matrix products, arithmetic and copies ran while one was open for 2% of the time, Pallas kernels for 13%

profile of v1, /device:TPU:0, one launch (start us, length us, event | category | flops | bytes accessed | tf_op | source)
XLA Modules:
  0.0 32.7 jit_solution(4547808404009160844)
XLA Ops:
  0.6 0.0 copy-start.1
  0.6 1.0 %copy-done.1 = bf16[1,128,2048]{2,1,0:T(8,128)(2,1)S(1)} copy-done((bf16[1,128,2048]{2,1,0:T(8,128)(2,1)S(1)}, bf16[1,128,2048]{2,1,0:T(8,128)(2,1)}, u32[]{:S(2)}) %copy-start.1) | copy-done | bytes 524312
  1.7 0.0 copy-start.2
  1.7 0.8 %copy-done.2 = bf16[1,1,16,1792]{3,2,1,0:T(8,128)(2,1)S(1)} copy-done((bf16[1,1,16,1792]{3,2,1,0:T(8,128)(2,1)S(1)}, bf16[1,1,16,1792]{3,2,1,0:T(8,128)(2,1)}, u32[]{:S(2)}) %copy-start.2) | copy-done | bytes 57368
  2.5 0.0 copy-start.3
  2.5 0.7 %copy-done.3 = s32[1,2,16]{2,1,0:T(2,128)S(1)} copy-done((s32[1,2,16]{2,1,0:T(2,128)S(1)}, s32[1,2,16]{2,1,0:T(2,128)}, u32[]{:S(2)}) %copy-start.3) | copy-done | bytes 152
  3.2 0.0 copy-start.5
  3.2 0.7 %copy-done.5 = f32[1,2,16]{2,1,0:T(2,128)S(1)} copy-done((f32[1,2,16]{2,1,0:T(2,128)S(1)}, f32[1,2,16]{2,1,0:T(2,128)}, u32[]{:S(2)}) %copy-start.5) | copy-done | bytes 152
  3.9 1.1 %prep.1 = (bf16[16,4,1024]{2,1,0:T(4,128)(2,1)}, bf16[32,1792]{1,0:T(8,128)(2,1)S(1)}) custom-call(s32[2,16]{1,0:T(2,128)S(1)} %bitcast.10, f32[2,16]{1,0:T(2,128)S(1)} %bitcast.12, bf16[16,1792]{1,0:T(8,128)(2,1)S(1)} %bitcast.9, bf16[128,2048]{1,0:T(8,128)(2,1)S(1)} %bitcast.8), custom_call_target="tpu_custom_call" | custom-call | flops 100000000 | bytes 1000000 | tf_op jit(solution)/shard_map/prep/pallas_call | solution.py:125
  4.9 7.4 %all-to-all-start.1 = ((bf16[16,4,1024]{2,1,0:T(4,128)(2,1)}), bf16[16,4,1024]{2,1,0:T(4,128)(2,1)S(1)}, u32[]{:S(2)}, u32[]{:S(2)}) async-start(bf16[16,4,1024]{2,1,0:T(4,128)(2,1)} %get-tuple-element.8), calls=%async_computation.1 | async-start | bytes 262144 | tf_op jit(solution)/shard_map/all_to_all | solution.py:112
  12.3 0.4 %collective-permute-start = (bf16[32,1792]{1,0:T(8,128)(2,1)S(1)}, bf16[32,1792]{1,0:T(8,128)(2,1)S(1)}, u32[]{:S(2)}, u32[]{:S(2)}) collective-permute-start(bf16[32,1792]{1,0:T(8,128)(2,1)S(1)} %get-tuple-element.6.own_ref), channel_id=1, source_target_pairs={{0,2},{2,0},{1,3},{3,1},{4,6},{6,4},{5,7},{7,5},{8,10},{10,8},{9,1... | collective-permute-start | bytes 344072 | tf_op jit(solution)/shard_map/ppermute | solution.py:137
  12.7 1.0 %collective-permute-done.other_ref = bf16[32,1792]{1,0:T(8,128)(2,1)S(1)} collective-permute-done((bf16[32,1792]{1,0:T(8,128)(2,1)S(1)}, bf16[32,1792]{1,0:T(8,128)(2,1)S(1)}, u32[]{:S(2)}, u32[]{:S(2)}) %collective-permute-start) | collective-permute-done | bytes 114720 | tf_op jit(solution)/shard_map/ppermute | solution.py:137
  13.8 0.0 copy-start
  13.8 2.0 %copy-done = bf16[1,1024,1792]{2,1,0:T(8,128)(2,1)S(1)} copy-done((bf16[1,1024,1792]{2,1,0:T(8,128)(2,1)S(1)}, bf16[1,1024,1792]{2,1,0:T(8,128)(2,1)}, u32[]{:S(2)}) %copy-start) | copy-done | bytes 3670040
  15.8 0.0 copy-start.4
  15.8 1.2 %partial.1 = (bf16[64,1024]{1,0:T(8,128)(2,1)S(1)}, bf16[64,1792]{1,0:T(8,128)(2,1)S(1)}) custom-call(bf16[32,1792]{1,0:T(8,128)(2,1)S(1)} %get-tuple-element.6.own_ref, bf16[32,1792]{1,0:T(8,128)(2,1)S(1)} %collective-permute-done.other_ref, bf16[1024,1792]{1,0:T(8,128)(2,1)S(1)} %bitcast.7), custom_call_target="tpu_custom_call" | custom-call | flops 1000000000 | bytes 4000000 | tf_op jit(solution)/shard_map/partial/pallas_call | solution.py:139
  17.0 0.7 %reshape.13 = bf16[16,4,1024]{2,1,0:T(4,128)(2,1)} reshape(bf16[64,1024]{1,0:T(8,128)(2,1)S(1)} %get-tuple-element.7) | data formatting | bytes 262144 | tf_op jit(solution)/shard_map/reshape | solution.py:151
  17.7 2.2 %all-to-all-done.1 = bf16[16,4,1024]{2,1,0:T(4,128)(2,1)S(1)} async-done(((bf16[16,4,1024]{2,1,0:T(4,128)(2,1)}), bf16[16,4,1024]{2,1,0:T(4,128)(2,1)S(1)}, u32[]{:S(2)}, u32[]{:S(2)}) %all-to-all-start.1) | async-done | bytes 131104 | tf_op jit(solution)/shard_map/all_to_all | solution.py:112
  20.0 3.7 %all-to-all-start = ((bf16[16,4,1024]{2,1,0:T(4,128)(2,1)}), bf16[16,4,1024]{2,1,0:T(4,128)(2,1)S(1)}, u32[]{:S(2)}, u32[]{:S(2)}) async-start(bf16[16,4,1024]{2,1,0:T(4,128)(2,1)} %reshape.13), calls=%async_computation | async-start | bytes 262144 | tf_op jit(solution)/shard_map/all_to_all | solution.py:112
  23.7 3.2 %weight_grad.1 = bf16[1024,1792]{1,0:T(8,128)(2,1)} custom-call(bf16[64,1024]{1,0:T(8,128)(2,1)S(1)} %reshape.15.rows_ref, bf16[64,1792]{1,0:T(8,128)(2,1)S(1)} %get-tuple-element.9.scaled_ref), custom_call_target="tpu_custom_call" | custom-call | flops 1000000000 | bytes 4000000 | tf_op jit(solution)/shard_map/weight_grad/pallas_call | solution.py:154
  26.9 4.4 %all-to-all-done = bf16[16,4,1024]{2,1,0:T(4,128)(2,1)S(1)} async-done(((bf16[16,4,1024]{2,1,0:T(4,128)(2,1)}), bf16[16,4,1024]{2,1,0:T(4,128)(2,1)S(1)}, u32[]{:S(2)}, u32[]{:S(2)}) %all-to-all-start) | async-done | bytes 131104 | tf_op jit(solution)/shard_map/all_to_all | solution.py:112
  31.3 0.0 copy-done.4
  31.3 1.4 %token_grad.1 = bf16[128,2048]{1,0:T(8,128)(2,1)} custom-call(s32[2,16]{1,0:T(2,128)S(1)} %bitcast.11, bf16[64,1024]{1,0:T(8,128)(2,1)S(1)} %reshape.14.parts_ref), custom_call_target="tpu_custom_call" | custom-call | flops 100000000 | bytes 1000000 | tf_op jit(solution)/shard_map/token_grad/pallas_call | solution.py:167
  (2 shorter events, 0.1 us)
Async XLA Ops:
  0.6 1.0 %copy-start.1 = (bf16[1,128,2048]{2,1,0:T(8,128)(2,1)S(1)}, bf16[1,128,2048]{2,1,0:T(8,128)(2,1)}, u32[]{:S(2)}) copy-start(bf16[1,128,2048]{2,1,0:T(8,128)(2,1)} %param.5) | copy-start | bytes 1572868
  1.7 0.8 %copy-start.2 = (bf16[1,1,16,1792]{3,2,1,0:T(8,128)(2,1)S(1)}, bf16[1,1,16,1792]{3,2,1,0:T(8,128)(2,1)}, u32[]{:S(2)}) copy-start(bf16[1,1,16,1792]{3,2,1,0:T(8,128)(2,1)} %param.7) | copy-start | bytes 172036
  2.5 0.7 %copy-start.3 = (s32[1,2,16]{2,1,0:T(2,128)S(1)}, s32[1,2,16]{2,1,0:T(2,128)}, u32[]{:S(2)}) copy-start(s32[1,2,16]{2,1,0:T(2,128)} %param.9) | copy-start | bytes 388
  3.2 0.7 %copy-start.5 = (f32[1,2,16]{2,1,0:T(2,128)S(1)}, f32[1,2,16]{2,1,0:T(2,128)}, u32[]{:S(2)}) copy-start(f32[1,2,16]{2,1,0:T(2,128)} %param.8) | copy-start | bytes 388
  4.9 15.0 %all-to-all-start.1 = ((bf16[16,4,1024]{2,1,0:T(4,128)(2,1)}), bf16[16,4,1024]{2,1,0:T(4,128)(2,1)S(1)}, u32[]{:S(2)}, u32[]{:S(2)}) async-start(bf16[16,4,1024]{2,1,0:T(4,128)(2,1)} %get-tuple-element.8), calls=%async_computation.1 | async-start | bytes 262144 | tf_op jit(solution)/shard_map/all_to_all | solution.py:112
  12.3 1.4 %collective-permute-start = (bf16[32,1792]{1,0:T(8,128)(2,1)S(1)}, bf16[32,1792]{1,0:T(8,128)(2,1)S(1)}, u32[]{:S(2)}, u32[]{:S(2)}) collective-permute-start(bf16[32,1792]{1,0:T(8,128)(2,1)S(1)} %get-tuple-element.6.own_ref), channel_id=1, source_target_pairs={{0,2},{2,0},{1,3},{3,1},{4,6},{6,4},{5,7},{7,5},{8,10},{10,8},{9,1... | collective-permute-start | bytes 344072 | tf_op jit(solution)/shard_map/ppermute | solution.py:137
  13.8 2.0 %copy-start = (bf16[1,1024,1792]{2,1,0:T(8,128)(2,1)S(1)}, bf16[1,1024,1792]{2,1,0:T(8,128)(2,1)}, u32[]{:S(2)}) copy-start(bf16[1,1024,1792]{2,1,0:T(8,128)(2,1)} %param.6) | copy-start | bytes 11010052
  15.8 15.5 %copy-start.4 = (s32[1,2,16]{2,1,0:T(2,128)S(1)}, s32[1,2,16]{2,1,0:T(2,128)}, u32[]{:S(2)}) copy-start(s32[1,2,16]{2,1,0:T(2,128)} %param.9) | copy-start | bytes 388
  20.0 11.3 %all-to-all-start = ((bf16[16,4,1024]{2,1,0:T(4,128)(2,1)}), bf16[16,4,1024]{2,1,0:T(4,128)(2,1)S(1)}, u32[]{:S(2)}, u32[]{:S(2)}) async-start(bf16[16,4,1024]{2,1,0:T(4,128)(2,1)} %reshape.13), calls=%async_computation | async-start | bytes 262144 | tf_op jit(solution)/shard_map/all_to_all | solution.py:112

commit v2 on v1

v2 whole, which is shorter than its diff:
```python
import functools

import jax
import jax.numpy as jnp
from jax import lax
from jax.experimental import pallas as pl
from jax.experimental.pallas import tpu as pltpu
from jax.sharding import PartitionSpec as P

MOST = 4
BLOCK = 2 * MOST
BF16 = jnp.bfloat16
F32 = jnp.float32
VMEM = pl.BlockSpec(memory_space=pltpu.VMEM)
HBM = pl.BlockSpec(memory_space=pltpu.HBM)
DMA = pltpu.SemaphoreType.DMA


def params(limit_mib=24):
    return pltpu.CompilerParams(vmem_limit_bytes=limit_mib * 2**20)


def cost(flops, moved):
    return pl.CostEstimate(flops=flops, bytes_accessed=moved, transcendentals=0)


def to_column(row):
    n = row.shape[1]
    eye = lax.broadcasted_iota(jnp.int32, (n, n), 0) == lax.broadcasted_iota(jnp.int32, (n, n), 1)
    return jnp.sum(jnp.where(eye, row, jnp.zeros_like(row)), axis=1, keepdims=True)


def owner_and_arrival(chosen, tok_dev):
    n = chosen.shape[1]
    owner = chosen // tok_dev
    before = lax.broadcasted_iota(jnp.int32, (n, n), 0) < lax.broadcasted_iota(jnp.int32, (n, n), 1)
    same = to_column(owner) == owner
    arrival = jnp.sum(jnp.where(same & before, 1, 0), axis=0, keepdims=True)
    return owner, arrival


def own_rows(chosen_ref, owner_id, tok_dev):
    out = []
    for e in range(chosen_ref.shape[0]):
        chosen = chosen_ref[e : e + 1, :]
        owner, arrival = owner_and_arrival(chosen, tok_dev)
        place = jnp.where(owner == owner_id, arrival, -1)
        hit = lax.broadcasted_iota(jnp.int32, (MOST, chosen.shape[1]), 0) == place
        out.append(jnp.sum(jnp.where(hit, chosen - owner * tok_dev + 1, 0), axis=1, keepdims=True))
    return out


def as_onehot(mask):
    return mask.astype(F32).astype(BF16)


def spread(chosen, owners, tok_dev, offset):
    owner, arrival = owner_and_arrival(chosen, tok_dev)
    shape = (owners * BLOCK, chosen.shape[1])
    return as_onehot(lax.broadcasted_iota(jnp.int32, shape, 0) == owner * BLOCK + arrival + offset)


def gated(gate_row, grads):
    return (to_column(gate_row) * grads.astype(F32)).astype(BF16)


def prep_kernel(
    n_expert,
    n_tensor,
    n_data,
    chosen_hbm,
    gate_hbm,
    grads_hbm,
    tokens_hbm,
    weight_hbm,
    weight_ref,
    send_ref,
    scaled_ref,
    placed_ref,
    spread_ref,
    hits_ref,
    chosen_ref,
    gate_ref,
    grads_ref,
    tokens_ref,
    sems,
):
    loads = [
        pltpu.make_async_copy(src, dst, sems.at[i])
        for i, (src, dst) in enumerate(
            (
                (chosen_hbm, chosen_ref),
                (gate_hbm, gate_ref),
                (grads_hbm, grads_ref),
                (tokens_hbm, tokens_ref),
                (weight_hbm, weight_ref),
            )
        )
    ]
    for load in loads:
        load.start()
    tok_dev, features = tokens_ref.shape
    experts = chosen_ref.shape[0]
    halves = n_expert // experts
    owners = n_expert * n_tensor
    share = features // n_data
    own_half = lax.axis_index("expert")
    owner_id = own_half * n_tensor + lax.axis_index("tensor")
    own_expert = own_half // halves
    loads[0].wait()
    target = own_rows(chosen_ref, owner_id, tok_dev)
    empty = jnp.zeros((MOST, 1), jnp.int32)
    outgoing = jnp.concatenate([t for e in range(experts) for t in (target[e], empty) * (halves * n_tensor)], axis=0)
    incoming = jnp.concatenate([t for e in range(experts) for t in (empty, target[e]) * (halves * n_tensor)], axis=0)
    rows = lax.broadcasted_iota(jnp.int32, (owners * BLOCK, tok_dev), 1) + 1
    hits_ref[...] = as_onehot(rows == incoming)
    pick = as_onehot(rows == outgoing)
    chosen = chosen_ref[pl.ds(own_expert, 1), :]
    spread_ref[...] = spread(chosen, owners, tok_dev, MOST)
    loads[1].wait()
    loads[2].wait()
    scaled = gated(gate_ref[pl.ds(own_expert, 1), :], grads_ref[...])
    scaled_ref[...] = scaled
    placed_ref[...] = jnp.dot(
        spread(chosen, owners, tok_dev, 0), scaled, preferred_element_type=F32
    ).astype(BF16)
    loads[3].wait()
    for d in range(n_data):
        send_ref[d * owners * BLOCK : (d + 1) * owners * BLOCK, :] = jnp.dot(
            pick, tokens_ref[:, d * share : (d + 1) * share], preferred_element_type=F32
        ).astype(BF16)
    loads[4].wait()


def partial_kernel(
    n_expert,
    n_tensor,
    tok_dev,
    chosen_ref,
    gate_ref,
    grads_ref,
    weight_ref,
    rows_ref,
    scaled_ref,
    placed_ref,
    spread_ref,
    send_ref,
    all_ref,
):
    owners = n_expert * n_tensor
    places = owners * BLOCK
    halves = n_expert // chosen_ref.shape[0]
    capacity = chosen_ref.shape[1]
    own_expert = lax.axis_index("expert") // halves
    group = lax.axis_index("dp")
    mine = pl.ds(pl.multiple_of(group * places, places), places)
    theirs = pl.ds(pl.multiple_of((1 - group) * places, places), places)
    chosen = chosen_ref[pl.ds(own_expert, 1), :]
    scaled = gated(gate_ref[pl.ds(own_expert, 1), :], grads_ref[...])
    part = lax.dot_general(
        jnp.concatenate([scaled_ref[...], scaled], axis=0),
        weight_ref[...],
        (((1,), (1,)), ((), ())),
        preferred_element_type=F32,
    ).astype(BF16)
    put = spread(chosen, owners, tok_dev, MOST)
    for where, place, piece in ((mine, spread_ref[...], part[:capacity]), (theirs, put, part[capacity:])):
        out = jnp.dot(place, piece, preferred_element_type=F32)
        send_ref[where, :] = (out + rows_ref[where, :].astype(F32)).astype(BF16)
    all_ref[mine, :] = placed_ref[...]
    all_ref[theirs, :] = jnp.dot(
        spread(chosen, owners, tok_dev, 0), scaled, preferred_element_type=F32
    ).astype(BF16)


def finish_kernel(
    n_data, chunk, arrived_ref, scaled_ref, hits_ref, weight_hbm, token_hbm, weight_buf, token_buf, weight_sems, token_sem
):
    share, hidden = weight_hbm.shape
    places = hits_ref.shape[0]
    stores = []
    for i in range(share // chunk):
        here = slice(i * chunk, (i + 1) * chunk)
        weight_buf[here, :] = lax.dot_general(
            arrived_ref[:, here], scaled_ref[...], (((0,), (0,)), ((), ())), preferred_element_type=F32
        ).astype(BF16)
        stores.append(pltpu.make_async_copy(weight_buf.at[here, :], weight_hbm.at[here, :], weight_sems.at[i]))
        stores[-1].start()
    for d in range(n_data):
        token_buf[:, d * share : (d + 1) * share] = lax.dot_general(
            hits_ref[...],
            arrived_ref[d * places : (d + 1) * places, :],
            (((0,), (0,)), ((), ())),
            preferred_element_type=F32,
        ).astype(BF16)
    stores.append(pltpu.make_async_copy(token_buf, token_hbm, token_sem))
    stores[-1].start()
    for store in stores:
        store.wait()


def local(tokens, proj_weight, slot_grads, gate_weights, selected):
    n_tensor = lax.axis_size("tensor")
    n_expert = lax.axis_size("expert")
    n_data = lax.axis_size("dp")
    owners = n_expert * n_tensor
    members = owners * n_data
    places = owners * BLOCK
    tok_dev, features = tokens.shape[1:]
    hidden = proj_weight.shape[2]
    experts, capacity = selected.shape[1:]
    share = features // n_data
    chosen, gate, grads = selected[0], gate_weights[0], slot_grads[0, 0]
    swap = [(0, 1), (1, 0)]
    other_grads = lax.ppermute(grads, "dp", swap)
    other_chosen = lax.ppermute(chosen, "dp", swap)
    other_gate = lax.ppermute(gate, "dp", swap)
    weight, rows, scaled, placed, spread_own, hits = pl.pallas_call(
        functools.partial(prep_kernel, n_expert, n_tensor, n_data),
        out_shape=(
            jax.ShapeDtypeStruct((share, hidden), BF16),
            jax.ShapeDtypeStruct((n_data * places, share), BF16),
            jax.ShapeDtypeStruct((capacity, hidden), BF16),
            jax.ShapeDtypeStruct((places, hidden), BF16),
            jax.ShapeDtypeStruct((places, capacity), BF16),
            jax.ShapeDtypeStruct((places, tok_dev), BF16),
        ),
        in_specs=[HBM] * 5,
        out_specs=(VMEM,) * 6,
        scratch_shapes=[
            pltpu.VMEM((experts, capacity), jnp.int32),
            pltpu.VMEM((experts, capacity), F32),
            pltpu.VMEM((capacity, hidden), BF16),
            pltpu.VMEM((tok_dev, features), BF16),
            DMA((5,)),
        ],
        compiler_params=params(),
        cost_estimate=cost(10**8, 5 * 10**6),
        name="prep",
    )(*(pltpu.with_memory_space_constraint(x, pltpu.HBM) for x in (chosen, gate, grads, tokens[0], proj_weight[0])))
    send, scaled_all = pl.pallas_call(
        functools.partial(partial_kernel, n_expert, n_tensor, tok_dev),
        out_shape=(
            jax.ShapeDtypeStruct((n_data * places, share), BF16),
            jax.ShapeDtypeStruct((n_data * places, hidden), BF16),
        ),
        in_specs=[VMEM] * 8,
        out_specs=(VMEM, VMEM),
        compiler_params=params(),
        cost_estimate=cost(10**9, 4 * 10**6),
        name="partial",
    )(other_chosen, other_gate, other_grads, weight, rows, scaled, placed, spread_own)
    arrived = lax.all_to_all(
        send.reshape(members, BLOCK, share), ("dp", "expert", "tensor"), split_axis=0, concat_axis=0, tiled=True
    )
    chunk = min(128, share)
    weight_grads, token_grads = pl.pallas_call(
        functools.partial(finish_kernel, n_data, chunk),
        out_shape=(
            jax.ShapeDtypeStruct((share, hidden), BF16),
            jax.ShapeDtypeStruct((tok_dev, features), BF16),
        ),
        in_specs=[VMEM] * 3,
        out_specs=(HBM, HBM),
        scratch_shapes=[
            pltpu.VMEM((share, hidden), BF16),
            pltpu.VMEM((tok_dev, features), BF16),
            DMA((share // chunk,)),
            DMA,
        ],
        compiler_params=params(),
        cost_estimate=cost(10**9, 4 * 10**6),
        name="finish",
    )(arrived.reshape(n_data * places, share), scaled_all, hits)
    return token_grads[None], weight_grads[None]


def solution(mesh):
    in_specs = (
        P("dp", ("groups", "expert", "tensor"), None),
        P("expert", "dp", "tensor"),
        P("dp", "expert", "groups", "tensor"),
        P("dp", None, "groups"),
        P("dp", None, "groups"),
    )
    out_specs = (
        P("dp", ("groups", "expert", "tensor"), None),
        P(("groups", "expert"), "dp", "tensor"),
    )
    return jax.shard_map(local, mesh=mesh, in_specs=in_specs, out_specs=out_specs, check_vma=False)
```

time: 33.2 us -> 25.2 us (0.76)
  blocking collectives: 0 us -> 17.1 us
  starting transfers between devices: 11.5 us -> 1.07 us
  waiting for transfers between devices: 7.67 us -> 0.01 us
  local copies, waits for them, and re-layouts: 6.03 us -> 0 us
  Pallas kernels: 6.86 us -> 6.14 us
    all_to_all x0 -> x1, blocking collectives: none -> 17.1 us  [local(): lax.all_to_all(send.reshape(members, BLOCK, share), ('dp', 'expert', 'ten...]
    all_to_all x2 -> x0, starting transfers between devices: 11.1 us -> none  [exchange(): lax.all_to_all(blocks, ('dp', 'expert', 'tensor'), split_axis=0, concat_a...]
    all_to_all x2 -> x0, waiting for transfers between devices: 6.64 us -> none  [exchange(): lax.all_to_all(blocks, ('dp', 'expert', 'tensor'), split_axis=0, concat_a...]
    unnamed x12 -> x0, local copies, waits for them, and re-layouts: 5.25 us -> none
    ppermute x1 -> x3, waiting for transfers between devices: 1.03 us -> 0.01 us  [the longest x1 0.01 us: local(): other_gate = lax.ppermute(gate, 'dp', swap)]
    reshape x3 -> x0, local copies, waits for them, and re-layouts: 0.78 us -> none  [the longest x1 0.71 us: local(): returned = exchange(part.reshape(members, MOST, share))]
    pallas_call x4 -> x3, Pallas kernels: 6.86 us -> 6.14 us  [the longest x1 2.41 us: local(): pl.pallas_call(functools.partial(finish_kernel, n_data, chunk), out_shape...]
    ppermute x1 -> x3, starting transfers between devices: 0.41 us -> 1.07 us  [the longest x1 0.56 us: local(): other_grads = lax.ppermute(grads, 'dp', swap)]
  transfers between devices with their start and end apart: 3 -> 3, of which waited for: 3 -> 0; matrix products, arithmetic and copies ran while one was open for 2% -> 0% of each run, Pallas kernels for 13% -> 9%
where the time goes in v2:
time: 25.2 us; the launch traced here: 25 us
  blocking collectives  17.1 us (68%)
  Pallas kernels  6.14 us (24%)
  starting transfers between devices  1.07 us (4%)
  between operations  0.67 us (3%)
    all_to_all x1, blocking collectives, local(): lax.all_to_all(send.reshape(members, BLOCK, share), ('dp', 'expert', 'ten...  17.1 us
    pallas_call x1, Pallas kernels, local(): pl.pallas_call(functools.partial(finish_kernel, n_data, chunk), out_shape...  2.41 us
    pallas_call x1, Pallas kernels, local(): pl.pallas_call(functools.partial(prep_kernel, n_expert, n_tensor, n_data)...  2.3 us
    pallas_call x1, Pallas kernels, local(): pl.pallas_call(functools.partial(partial_kernel, n_expert, n_tensor, tok_...  1.42 us
    ppermute x1, starting transfers between devices, local(): other_grads = lax.ppermute(grads, 'dp', swap)  0.56 us
  transfers between devices with their start and end apart: 3, of which 0 were waited for; matrix products, arithmetic and copies ran while one was open for 0% of the time, Pallas kernels for 9%

profile of v2, /device:TPU:0, one launch (start us, length us, event | category | flops | bytes accessed | tf_op | source)
XLA Modules:
  0.0 25.0 jit_solution(13144484045524716866)
XLA Ops:
  0.6 0.6 %collective-permute-start.2 = (bf16[16,1792]{1,0:T(8,128)(2,1)}, bf16[16,1792]{1,0:T(8,128)(2,1)S(1)}, u32[]{:S(2)}, u32[]{:S(2)}) collective-permute-start(bf16[16,1792]{1,0:T(8,128)(2,1)} %bitcast.13), channel_id=1, source_target_pairs={{0,2},{2,0},{1,3},{3,1},{4,6},{6,4},{5,7},{7,5},{8,10},{10,8},{9,1... | collective-permute-start | bytes 172040 | tf_op jit(solution)/shard_map/ppermute | solution.py:215
  1.2 0.1 collective-permute-start.1
  1.3 0.4 %collective-permute-start = (s32[2,16]{1,0:T(2,128)}, s32[2,16]{1,0:T(2,128)S(1)}, u32[]{:S(2)}, u32[]{:S(2)}) collective-permute-start(s32[2,16]{1,0:T(2,128)} %bitcast.17), channel_id=1, source_target_pairs={{0,2},{2,0},{1,3},{3,1},{4,6},{6,4},{5,7},{7,5},{8,10},{10,8},{9,1... | collective-permute-start | bytes 392 | tf_op jit(solution)/shard_map/ppermute | solution.py:216
  1.7 2.3 %prep.1 = (bf16[1024,1792]{1,0:T(8,128)(2,1)S(1)}, bf16[128,1024]{1,0:T(8,128)(2,1)S(1)}, bf16[16,1792]{1,0:T(8,128)(2,1)S(1)}, bf16[64,1792]{1,0:T(8,128)(2,1)S...) custom-call(s32[2,16]{1,0:T(2,128)} %bitcast.18, f32[2,16]{1,0:T(2,128)} %bitcast.16, ...), custom_call_target="tpu_custom_call" | custom-call | flops 100000000 | bytes 5000000 | tf_op jit(solution)/shard_map/prep/pallas_call | solution.py:218
  4.0 0.0 collective-permute-done.1.gate_ref
  4.0 0.0 collective-permute-done.chosen_ref
  4.0 0.0 collective-permute-done.2.grads_ref
  4.0 1.4 %partial.1 = (bf16[128,1024]{1,0:T(8,128)(2,1)S(1)}, bf16[128,1792]{1,0:T(8,128)(2,1)S(1)}) custom-call(s32[2,16]{1,0:T(2,128)S(1)} %collective-permute-done.chosen_ref, f32[2,16]{1,0:T(2,128)S(1)} %collective-permute-done.1.gate_ref, bf16[16,1792]{1,0:T(8,128)(2,1)S(1)} %collective-permute-done.2.grads_ref, ...), custom_call_target="tpu_custom_call" | custom-call | flops 1000000000 | bytes 4000000 | tf_op jit(solution)/shard_map/partial/pallas_call | solution.py:241
  5.5 17.1 %all_to_all.5 = bf16[16,8,1024]{2,1,0:T(8,128)(2,1)S(1)} all-to-all(bf16[16,8,1024]{2,1,0:T(8,128)(2,1)S(1)} %bitcast.9), channel_id=1, replica_groups=mesh['groups'=2,'expert'=4,'dp'=2,'tensor'=2] {'dp','expert','tensor'}, dimensions={0} | all-to-all | bytes 524288 | tf_op jit(solution)/shard_map/all_to_all | solution.py:253
  22.6 2.4 %finish.1 = (bf16[1024,1792]{1,0:T(8,128)(2,1)}, bf16[128,2048]{1,0:T(8,128)(2,1)}) custom-call(bf16[128,1024]{1,0:T(8,128)(2,1)S(1)} %bitcast.10, bf16[128,1792]{1,0:T(8,128)(2,1)S(1)} %get-tuple-element.18.scaled_ref, bf16[64,128]{1,0:T(8,128)(2,1)S(1)} %get-tuple-element.19.hits_ref), custom_call_target="tpu_custom_call" | custom-call | flops 1000000000 | bytes 4000000 | tf_op jit(solution)/shard_map/finish/pallas_call | solution.py:257
Async XLA Ops:
  0.6 3.4 %collective-permute-start.2 = (bf16[16,1792]{1,0:T(8,128)(2,1)}, bf16[16,1792]{1,0:T(8,128)(2,1)S(1)}, u32[]{:S(2)}, u32[]{:S(2)}) collective-permute-start(bf16[16,1792]{1,0:T(8,128)(2,1)} %bitcast.13), channel_id=1, source_target_pairs={{0,2},{2,0},{1,3},{3,1},{4,6},{6,4},{5,7},{7,5},{8,10},{10,8},{9,1... | collective-permute-start | bytes 172040 | tf_op jit(solution)/shard_map/ppermute | solution.py:215
  1.2 2.8 %collective-permute-start.1 = (f32[2,16]{1,0:T(2,128)}, f32[2,16]{1,0:T(2,128)S(1)}, u32[]{:S(2)}, u32[]{:S(2)}) collective-permute-start(f32[2,16]{1,0:T(2,128)} %bitcast.15), channel_id=1, source_target_pairs={{0,2},{2,0},{1,3},{3,1},{4,6},{6,4},{5,7},{7,5},{8,10},{10,8},{9,1... | collective-permute-start | bytes 392 | tf_op jit(solution)/shard_map/ppermute | solution.py:217
  1.3 2.8 %collective-permute-start = (s32[2,16]{1,0:T(2,128)}, s32[2,16]{1,0:T(2,128)S(1)}, u32[]{:S(2)}, u32[]{:S(2)}) collective-permute-start(s32[2,16]{1,0:T(2,128)} %bitcast.17), channel_id=1, source_target_pairs={{0,2},{2,0},{1,3},{3,1},{4,6},{6,4},{5,7},{7,5},{8,10},{10,8},{9,1... | collective-permute-start | bytes 392 | tf_op jit(solution)/shard_map/ppermute | solution.py:216

commit v3 on v2

--- a/solution.py
+++ b/solution.py
@@ -39,15 +39,16 @@
     return owner, arrival
 
 
-def own_rows(chosen_ref, owner_id, tok_dev):
-    out = []
+def own_places(chosen_ref, gate_ref, owner_id, tok_dev):
+    targets, gates = [], []
     for e in range(chosen_ref.shape[0]):
         chosen = chosen_ref[e : e + 1, :]
         owner, arrival = owner_and_arrival(chosen, tok_dev)
         place = jnp.where(owner == owner_id, arrival, -1)
         hit = lax.broadcasted_iota(jnp.int32, (MOST, chosen.shape[1]), 0) == place
-        out.append(jnp.sum(jnp.where(hit, chosen - owner * tok_dev + 1, 0), axis=1, keepdims=True))
-    return out
+        targets.append(jnp.sum(jnp.where(hit, chosen - owner * tok_dev + 1, 0), axis=1, keepdims=True))
+        gates.append(jnp.sum(jnp.where(hit, gate_ref[e : e + 1, :], 0.0), axis=1, keepdims=True))
+    return targets, gates
 
 
 def as_onehot(mask):
@@ -58,10 +59,6 @@
     owner, arrival = owner_and_arrival(chosen, tok_dev)
     shape = (owners * BLOCK, chosen.shape[1])
     return as_onehot(lax.broadcasted_iota(jnp.int32, shape, 0) == owner * BLOCK + arrival + offset)
-
-
-def gated(gate_row, grads):
-    return (to_column(gate_row) * grads.astype(F32)).astype(BF16)
 
 
 def prep_kernel(
@@ -72,64 +69,60 @@
     gate_hbm,
     grads_hbm,
     tokens_hbm,
-    weight_hbm,
-    weight_ref,
     send_ref,
-    scaled_ref,
+    grads_ref,
     placed_ref,
     spread_ref,
     hits_ref,
     chosen_ref,
     gate_ref,
-    grads_ref,
     tokens_ref,
     sems,
 ):
-    loads = [
-        pltpu.make_async_copy(src, dst, sems.at[i])
-        for i, (src, dst) in enumerate(
-            (
-                (chosen_hbm, chosen_ref),
-                (gate_hbm, gate_ref),
-                (grads_hbm, grads_ref),
-                (tokens_hbm, tokens_ref),
-                (weight_hbm, weight_ref),
-            )
-        )
-    ]
+    pairs = (
+        (chosen_hbm, chosen_ref),
+        (gate_hbm, gate_ref),
+        (grads_hbm, grads_ref),
+        (tokens_hbm, tokens_ref),
+    )
+    loads = [pltpu.make_async_copy(src, dst, sems.at[i]) for i, (src, dst) in enumerate(pairs)]
     for load in loads:
         load.start()
     tok_dev, features = tokens_ref.shape
     experts = chosen_ref.shape[0]
     halves = n_expert // experts
     owners = n_expert * n_tensor
+    places = owners * BLOCK
     share = features // n_data
     own_half = lax.axis_index("expert")
     owner_id = own_half * n_tensor + lax.axis_index("tensor")
     own_expert = own_half // halves
     loads[0].wait()
-    target = own_rows(chosen_ref, owner_id, tok_dev)
-    empty = jnp.zeros((MOST, 1), jnp.int32)
-    outgoing = jnp.concatenate([t for e in range(experts) for t in (target[e], empty) * (halves * n_tensor)], axis=0)
-    incoming = jnp.concatenate([t for e in range(experts) for t in (empty, target[e]) * (halves * n_tensor)], axis=0)
-    rows = lax.broadcasted_iota(jnp.int32, (owners * BLOCK, tok_dev), 1) + 1
-    hits_ref[...] = as_onehot(rows == incoming)
-    pick = as_onehot(rows == outgoing)
+    loads[1].wait()
+    targets, gates = own_places(chosen_ref, gate_ref, owner_id, tok_dev)
+
+    def column(pieces, first):
+        none = jnp.zeros_like(pieces[0])
+        both = [(p, none) if first else (none, p) for p in pieces]
+        return jnp.concatenate([t for pair in both for t in pair * (halves * n_tensor)], axis=0)
+
+    rows = lax.broadcasted_iota(jnp.int32, (places, tok_dev), 1) + 1
+    weighted = jnp.where(rows == column(targets, False), column(gates, False), 0.0)
+    high = weighted.astype(BF16)
+    hits_ref[:places, :] = high
+    hits_ref[places:, :] = (weighted - high.astype(F32)).astype(BF16)
+    pick = as_onehot(rows == column(targets, True))
+    gate = column(gates, True)
     chosen = chosen_ref[pl.ds(own_expert, 1), :]
     spread_ref[...] = spread(chosen, owners, tok_dev, MOST)
-    loads[1].wait()
     loads[2].wait()
-    scaled = gated(gate_ref[pl.ds(own_expert, 1), :], grads_ref[...])
-    scaled_ref[...] = scaled
     placed_ref[...] = jnp.dot(
-        spread(chosen, owners, tok_dev, 0), scaled, preferred_element_type=F32
+        spread(chosen, owners, tok_dev, 0), grads_ref[...], preferred_element_type=F32
     ).astype(BF16)
     loads[3].wait()
     for d in range(n_data):
-        send_ref[d * owners * BLOCK : (d + 1) * owners * BLOCK, :] = jnp.dot(
-            pick, tokens_ref[:, d * share : (d + 1) * share], preferred_element_type=F32
-        ).astype(BF16)
-    loads[4].wait()
+        picked = jnp.dot(pick, tokens_ref[:, d * share : (d + 1) * share], preferred_element_type=F32)
+        send_ref[d * places : (d + 1) * places, :] = (gate * picked).astype(BF16)
 
 
 def partial_kernel(
@@ -137,11 +130,10 @@
     n_tensor,
     tok_dev,
     chosen_ref,
-    gate_ref,
-    grads_ref,
+    other_ref,
     weight_ref,
     rows_ref,
-    scaled_ref,
+    grads_ref,
     placed_ref,
     spread_ref,
     send_ref,
@@ -156,9 +148,9 @@
     mine = pl.ds(pl.multiple_of(group * places, places), places)
     theirs = pl.ds(pl.multiple_of((1 - group) * places, places), places)
     chosen = chosen_ref[pl.ds(own_expert, 1), :]
-    scaled = gated(gate_ref[pl.ds(own_expert, 1), :], grads_ref[...])
+    other = other_ref[...]
     part = lax.dot_general(
-        jnp.concatenate([scaled_ref[...], scaled], axis=0),
+        jnp.concatenate([grads_ref[...], other], axis=0),
         weight_ref[...],
         (((1,), (1,)), ((), ())),
         preferred_element_type=F32,
@@ -169,7 +161,7 @@
         send_ref[where, :] = (out + rows_ref[where, :].astype(F32)).astype(BF16)
     all_ref[mine, :] = placed_ref[...]
     all_ref[theirs, :] = jnp.dot(
-        spread(chosen, owners, tok_dev, 0), scaled, preferred_element_type=F32
+        spread(chosen, owners, tok_dev, 0), other, preferred_element_type=F32
     ).astype(BF16)
 
 
@@ -177,7 +169,7 @@
     n_data, chunk, arrived_ref, scaled_ref, hits_ref, weight_hbm, token_hbm, weight_buf, token_buf, weight_sems, token_sem
 ):
     share, hidden = weight_hbm.shape
-    places = hits_ref.shape[0]
+    places = hits_ref.shape[0] // 2
     stores = []
     for i in range(share // chunk):
         here = slice(i * chunk, (i + 1) * chunk)
@@ -187,12 +179,12 @@
         stores.append(pltpu.make_async_copy(weight_buf.at[here, :], weight_hbm.at[here, :], weight_sems.at[i]))
         stores[-1].start()
     for d in range(n_data):
-        token_buf[:, d * share : (d + 1) * share] = lax.dot_general(
-            hits_ref[...],
-            arrived_ref[d * places : (d + 1) * places, :],
-            (((0,), (0,)), ((), ())),
-            preferred_element_type=F32,
-        ).astype(BF16)
+        piece = arrived_ref[d * places : (d + 1) * places, :]
+        total = sum(
+            lax.dot_general(hits, piece, (((0,), (0,)), ((), ())), preferred_element_type=F32)
+            for hits in (hits_ref[:places, :], hits_ref[places:, :])
+        )
+        token_buf[:, d * share : (d + 1) * share] = total.astype(BF16)
     stores.append(pltpu.make_async_copy(token_buf, token_hbm, token_sem))
     stores[-1].start()
     for store in stores:
@@ -214,42 +206,39 @@
     swap = [(0, 1), (1, 0)]
     other_grads = lax.ppermute(grads, "dp", swap)
     other_chosen = lax.ppermute(chosen, "dp", swap)
-    other_gate = lax.ppermute(gate, "dp", swap)
-    weight, rows, scaled, placed, spread_own, hits = pl.pallas_call(
+    rows, own_grads, placed, spread_own, hits = pl.pallas_call(
         functools.partial(prep_kernel, n_expert, n_tensor, n_data),
         out_shape=(
-            jax.ShapeDtypeStruct((share, hidden), BF16),
             jax.ShapeDtypeStruct((n_data * places, share), BF16),
             jax.ShapeDtypeStruct((capacity, hidden), BF16),
             jax.ShapeDtypeStruct((places, hidden), BF16),
             jax.ShapeDtypeStruct((places, capacity), BF16),
-            jax.ShapeDtypeStruct((places, tok_dev), BF16),
+            jax.ShapeDtypeStruct((2 * places, tok_dev), BF16),
         ),
-        in_specs=[HBM] * 5,
-        out_specs=(VMEM,) * 6,
+        in_specs=[HBM] * 4,
+        out_specs=(VMEM,) * 5,
         scratch_shapes=[
             pltpu.VMEM((experts, capacity), jnp.int32),
             pltpu.VMEM((experts, capacity), F32),
-            pltpu.VMEM((capacity, hidden), BF16),
             pltpu.VMEM((tok_dev, features), BF16),
-            DMA((5,)),
+            DMA((4,)),
         ],
         compiler_params=params(),
-        cost_estimate=cost(10**8, 5 * 10**6),
+        cost_estimate=cost(12 * 10**8, 10**6),
         name="prep",
-    )(*(pltpu.with_memory_space_constraint(x, pltpu.HBM) for x in (chosen, gate, grads, tokens[0], proj_weight[0])))
+    )(*(pltpu.with_memory_space_constraint(x, pltpu.HBM) for x in (chosen, gate, grads, tokens[0])))
     send, scaled_all = pl.pallas_call(
         functools.partial(partial_kernel, n_expert, n_tensor, tok_dev),
         out_shape=(
             jax.ShapeDtypeStruct((n_data * places, share), BF16),
             jax.ShapeDtypeStruct((n_data * places, hidden), BF16),
         ),
-        in_specs=[VMEM] * 8,
+        in_specs=[VMEM] * 7,
         out_specs=(VMEM, VMEM),
         compiler_params=params(),
         cost_estimate=cost(10**9, 4 * 10**6),
         name="partial",
-    )(other_chosen, other_gate, other_grads, weight, rows, scaled, placed, spread_own)
+    )(other_chosen, other_grads, proj_weight[0], rows, own_grads, placed, spread_own)
     arrived = lax.all_to_all(
         send.reshape(members, BLOCK, share), ("dp", "expert", "tensor"), split_axis=0, concat_axis=0, tiled=True
     )

time: 25.2 us -> 24.5 us (0.972)
  Pallas kernels: 6.14 us -> 5.57 us
  starting transfers between devices: 1.07 us -> 0.64 us
  blocking collectives: 17.1 us -> 17.4 us
    pallas_call x1, Pallas kernels: 2.3 us -> 1.74 us  [local(): pl.pallas_call(functools.partial(prep_kernel, n_expert, n_tensor, n_data)...]
    ppermute x1, starting transfers between devices: 0.56 us -> 0.08 us  [local(): other_grads = lax.ppermute(grads, 'dp', swap)]
    all_to_all x1, blocking collectives: 17.1 us -> 17.4 us  [local(): lax.all_to_all(send.reshape(members, BLOCK, share), ('dp', 'expert', 'ten...]
  transfers between devices with their start and end apart: 3 -> 2, of which waited for: 0 -> 0; matrix products, arithmetic and copies ran while one was open for 0% -> 0% of each run, Pallas kernels for 9% -> 7%
where the time goes in v3:
time: 24.5 us; the launch traced here: 24.3 us
  blocking collectives  17.4 us (71%)
  Pallas kernels  5.57 us (23%)
  between operations  0.68 us (3%)
  starting transfers between devices  0.64 us (3%)
    all_to_all x1, blocking collectives, local(): lax.all_to_all(send.reshape(members, BLOCK, share), ('dp', 'expert', 'ten...  17.4 us
    pallas_call x1, Pallas kernels, local(): pl.pallas_call(functools.partial(finish_kernel, n_data, chunk), out_shape...  2.4 us
    pallas_call x1, Pallas kernels, local(): pl.pallas_call(functools.partial(prep_kernel, n_expert, n_tensor, n_data)...  1.74 us
    pallas_call x1, Pallas kernels, local(): pl.pallas_call(functools.partial(partial_kernel, n_expert, n_tensor, tok_...  1.44 us
    ppermute x1, starting transfers between devices, local(): other_chosen = lax.ppermute(chosen, 'dp', swap)  0.56 us
  transfers between devices with their start and end apart: 2, of which 0 were waited for; matrix products, arithmetic and copies ran while one was open for 0% of the time, Pallas kernels for 7%

profile of v3, /device:TPU:0, one launch (start us, length us, event | category | flops | bytes accessed | tf_op | source)
XLA Modules:
  0.0 24.3 jit_solution(8791960769436869035)
XLA Ops:
  0.6 0.0 copy-start
  0.6 0.6 %collective-permute-start = (s32[2,16]{1,0:T(2,128)}, s32[2,16]{1,0:T(2,128)S(1)}, u32[]{:S(2)}, u32[]{:S(2)}) collective-permute-start(s32[2,16]{1,0:T(2,128)} %bitcast.16), channel_id=1, source_target_pairs={{0,2},{2,0},{1,3},{3,1},{4,6},{6,4},{5,7},{7,5},{8,10},{10,8},{9,1... | collective-permute-start | bytes 392 | tf_op jit(solution)/shard_map/ppermute | solution.py:208
  1.2 0.1 collective-permute-start.1
  1.3 1.7 %prep.1 = (bf16[128,1024]{1,0:T(8,128)(2,1)S(1)}, bf16[16,1792]{1,0:T(8,128)(2,1)S(1)}, bf16[64,1792]{1,0:T(8,128)(2,1)S(1)}, bf16[64,16]{1,0:T(8,128)(2,1)S(1)}, bf16[128,128]{1,0:T(8,128)(2,1)S(1)}) custom-call(s32[2,16]{1,0:T(2,128)} %bitcast.17, f32[2,16]{1,0:T(2,128)} %bitcast.15, bf16[16,1792]{1,0:T(8,128)(2,1)} %bitcast.14, bf16[128,2048]{1,0:T(8,128)(2,1)} %bitcast.12), custom_call_target="tpu_custom_call" | custom-call | flops 1200000000 | bytes 1000000 | tf_op jit(solution)/shard_map/prep/pallas_call | solution.py:209
  3.0 0.0 collective-permute-done.chosen_ref
  3.0 0.0 collective-permute-done.1.other_ref
  3.0 0.0 copy-done
  3.1 1.4 %partial.1 = (bf16[128,1024]{1,0:T(8,128)(2,1)S(1)}, bf16[128,1792]{1,0:T(8,128)(2,1)S(1)}) custom-call(s32[2,16]{1,0:T(2,128)S(1)} %collective-permute-done.chosen_ref, bf16[16,1792]{1,0:T(8,128)(2,1)S(1)} %collective-permute-done.1.other_ref, bf16[1024,1792]{1,0:T(8,128)(2,1)S(1)} %bitcast.9, bf16[128,1024]{1,0:T(8,128)(2,1)S(1)} %get-tuple-element.11.rows_ref, ...), custom_call_target="tpu_custom_call" | custom-call | flops 1000000000 | bytes 4000000 | tf_op jit(solution)/shard_map/partial/pallas_call | solution.py:230
  4.5 17.4 %all_to_all.5 = bf16[16,8,1024]{2,1,0:T(8,128)(2,1)S(1)} all-to-all(bf16[16,8,1024]{2,1,0:T(8,128)(2,1)S(1)} %bitcast.10), channel_id=1, replica_groups=mesh['groups'=2,'expert'=4,'dp'=2,'tensor'=2] {'dp','expert','tensor'}, dimensions={0} | all-to-all | bytes 524288 | tf_op jit(solution)/shard_map/all_to_all | solution.py:242
  21.9 2.4 %finish.1 = (bf16[1024,1792]{1,0:T(8,128)(2,1)}, bf16[128,2048]{1,0:T(8,128)(2,1)}) custom-call(bf16[128,1024]{1,0:T(8,128)(2,1)S(1)} %bitcast.11, bf16[128,1792]{1,0:T(8,128)(2,1)S(1)} %get-tuple-element.16.scaled_ref, bf16[128,128]{1,0:T(8,128)(2,1)S(1)} %get-tuple-element.17.hits_ref), custom_call_target="tpu_custom_call" | custom-call | flops 1000000000 | bytes 4000000 | tf_op jit(solution)/shard_map/finish/pallas_call | solution.py:246
Async XLA Ops:
  0.6 2.4 %copy-start = (bf16[1,1024,1792]{2,1,0:T(8,128)(2,1)S(1)}, bf16[1,1024,1792]{2,1,0:T(8,128)(2,1)}, u32[]{:S(2)}) copy-start(bf16[1,1024,1792]{2,1,0:T(8,128)(2,1)} %param.6) | copy-start | bytes 11010052
  0.6 2.4 %collective-permute-start = (s32[2,16]{1,0:T(2,128)}, s32[2,16]{1,0:T(2,128)S(1)}, u32[]{:S(2)}, u32[]{:S(2)}) collective-permute-start(s32[2,16]{1,0:T(2,128)} %bitcast.16), channel_id=1, source_target_pairs={{0,2},{2,0},{1,3},{3,1},{4,6},{6,4},{5,7},{7,5},{8,10},{10,8},{9,1... | collective-permute-start | bytes 392 | tf_op jit(solution)/shard_map/ppermute | solution.py:208
  1.2 1.8 %collective-permute-start.1 = (bf16[16,1792]{1,0:T(8,128)(2,1)}, bf16[16,1792]{1,0:T(8,128)(2,1)S(1)}, u32[]{:S(2)}, u32[]{:S(2)}) collective-permute-start(bf16[16,1792]{1,0:T(8,128)(2,1)} %bitcast.13), channel_id=1, source_target_pairs={{0,2},{2,0},{1,3},{3,1},{4,6},{6,4},{5,7},{7,5},{8,10},{10,8},{9,1... | collective-permute-start | bytes 172040 | tf_op jit(solution)/shard_map/ppermute | solution.py:207

commit v4 on v3

v4 whole, which is shorter than its diff:
```python
import functools
import math

import jax
import jax.numpy as jnp
from jax import lax
from jax.experimental import pallas as pl
from jax.experimental.pallas import tpu as pltpu
from jax.sharding import PartitionSpec as P

MOST = 4
BLOCK = 2 * MOST
STRIDE = 11
START = 12
BF16 = jnp.bfloat16
F32 = jnp.float32
VMEM = pl.BlockSpec(memory_space=pltpu.VMEM)
HBM = pl.BlockSpec(memory_space=pltpu.HBM)
DMA = pltpu.SemaphoreType.DMA


def params(limit_mib=24):
    return pltpu.CompilerParams(vmem_limit_bytes=limit_mib * 2**20)


def cost(flops, moved):
    return pl.CostEstimate(flops=flops, bytes_accessed=moved, transcendentals=0)


def exchange_order(n_expert, n_tensor, n_data):
    walk = [
        (d, h, t) for t in range(n_tensor) for h in range(n_expert) for d in reversed(range(n_data))
    ]
    n = len(walk)
    stride = STRIDE if math.gcd(STRIDE, n) == 1 else 1
    return [walk[(stride * k + START) % n] for k in range(n)]


def to_column(row):
    n = row.shape[1]
    eye = lax.broadcasted_iota(jnp.int32, (n, n), 0) == lax.broadcasted_iota(jnp.int32, (n, n), 1)
    return jnp.sum(jnp.where(eye, row, jnp.zeros_like(row)), axis=1, keepdims=True)


def owner_and_arrival(chosen, tok_dev):
    n = chosen.shape[1]
    owner = chosen // tok_dev
    before = lax.broadcasted_iota(jnp.int32, (n, n), 0) < lax.broadcasted_iota(jnp.int32, (n, n), 1)
    same = to_column(owner) == owner
    arrival = jnp.sum(jnp.where(same & before, 1, 0), axis=0, keepdims=True)
    return owner, arrival


def own_places(chosen_ref, gate_ref, slots, owner_id, tok_dev):
    targets, gates = [], []
    for e, (owner, arrival) in enumerate(slots):
        chosen = chosen_ref[e : e + 1, :]
        place = jnp.where(owner == owner_id, arrival, -1)
        hit = lax.broadcasted_iota(jnp.int32, (MOST, chosen.shape[1]), 0) == place
        targets.append(jnp.sum(jnp.where(hit, chosen - owner * tok_dev + 1, 0), axis=1, keepdims=True))
        gates.append(jnp.sum(jnp.where(hit, gate_ref[e : e + 1, :], 0.0), axis=1, keepdims=True))
    return targets, gates


def as_onehot(mask):
    return mask.astype(F32).astype(BF16)


def block_of(order, owner, group, n_tensor):
    out = jnp.zeros_like(owner)
    for k, (d, h, t) in enumerate(order):
        out = out + jnp.where((owner == h * n_tensor + t) & (group == d), k, 0)
    return out


def spread(place, blocks):
    return as_onehot(lax.broadcasted_iota(jnp.int32, (blocks * BLOCK, place.shape[1]), 0) == place)


def prep_kernel(
    order,
    n_expert,
    n_tensor,
    n_data,
    chosen_hbm,
    gate_hbm,
    grads_hbm,
    tokens_hbm,
    send_ref,
    grads_ref,
    placed_ref,
    place_ref,
    hits_ref,
    chosen_ref,
    gate_ref,
    tokens_ref,
    sems,
):
    pairs = (
        (chosen_hbm, chosen_ref),
        (gate_hbm, gate_ref),
        (grads_hbm, grads_ref),
        (tokens_hbm, tokens_ref),
    )
    loads = [pltpu.make_async_copy(src, dst, sems.at[i]) for i, (src, dst) in enumerate(pairs)]
    for load in loads:
        load.start()
    tok_dev, features = tokens_ref.shape
    experts = chosen_ref.shape[0]
    halves = n_expert // experts
    blocks = len(order)
    share = features // n_data
    own_half = lax.axis_index("expert")
    owner_id = own_half * n_tensor + lax.axis_index("tensor")
    own_expert = own_half // halves
    group = lax.axis_index("dp")
    loads[0].wait()
    loads[1].wait()
    slots = [owner_and_arrival(chosen_ref[e : e + 1, :], tok_dev) for e in range(experts)]
    owner = sum(jnp.where(own_expert == e, slot[0], 0) for e, slot in enumerate(slots))
    arrival = sum(jnp.where(own_expert == e, slot[1], 0) for e, slot in enumerate(slots))
    place = block_of(order, owner, group, n_tensor) * BLOCK + arrival
    place_ref[...] = place
    targets, gates = own_places(chosen_ref, gate_ref, slots, owner_id, tok_dev)
    none, no_gate = jnp.zeros_like(targets[0]), jnp.zeros_like(gates[0])
    rows = lax.broadcasted_iota(jnp.int32, (blocks * BLOCK, tok_dev), 1) + 1
    for side in range(n_data):
        ours = [h // halves if d == side else None for d, h, t in order]
        target = jnp.concatenate([p for e in ours for p in (none, none if e is None else targets[e])], axis=0)
        gate = jnp.concatenate([p for e in ours for p in (no_gate, no_gate if e is None else gates[e])], axis=0)
        weighted = jnp.where(rows == target, gate, 0.0)
        high = weighted.astype(BF16)
        hits_ref[side, 0] = high
        hits_ref[side, 1] = (weighted - high.astype(F32)).astype(BF16)
    rows = lax.broadcasted_iota(jnp.int32, (experts * BLOCK, tok_dev), 1) + 1
    pick = as_onehot(rows == jnp.concatenate([p for target in targets for p in (target, none)], axis=0))
    gate = jnp.concatenate([p for g in gates for p in (g, no_gate)], axis=0)
    loads[2].wait()
    placed_ref[...] = jnp.dot(spread(place, blocks), grads_ref[...], preferred_element_type=F32).astype(BF16)
    loads[3].wait()
    picked = gate * jnp.dot(pick, tokens_ref[...], preferred_element_type=F32)
    for k, (d, h, t) in enumerate(order):
        e = h // halves
        send_ref[k * BLOCK : (k + 1) * BLOCK, :] = picked[
            e * BLOCK : (e + 1) * BLOCK, d * share : (d + 1) * share
        ].astype(BF16)


def partial_kernel(
    order,
    n_expert,
    n_tensor,
    tok_dev,
    chosen_ref,
    other_ref,
    weight_ref,
    rows_ref,
    grads_ref,
    placed_ref,
    place_ref,
    send_ref,
    all_ref,
):
    blocks = len(order)
    halves = n_expert // chosen_ref.shape[0]
    capacity = chosen_ref.shape[1]
    own_expert = lax.axis_index("expert") // halves
    owner, arrival = owner_and_arrival(chosen_ref[pl.ds(own_expert, 1), :], tok_dev)
    place = block_of(order, owner, 1 - lax.axis_index("dp"), n_tensor) * BLOCK + arrival
    other = other_ref[...]
    part = lax.dot_general(
        jnp.concatenate([grads_ref[...], other], axis=0),
        weight_ref[...],
        (((1,), (1,)), ((), ())),
        preferred_element_type=F32,
    ).astype(BF16)
    out = rows_ref[...].astype(F32)
    for put, piece in ((place_ref[...], part[:capacity]), (place, part[capacity:])):
        out = out + jnp.dot(spread(put + MOST, blocks), piece, preferred_element_type=F32)
    send_ref[...] = out.astype(BF16)
    theirs = jnp.dot(spread(place, blocks), other, preferred_element_type=F32)
    all_ref[...] = (placed_ref[...].astype(F32) + theirs).astype(BF16)


def finish_kernel(
    n_data, chunk, arrived_ref, scaled_ref, hits_ref, weight_hbm, token_hbm, weight_buf, token_buf, weight_sems, token_sem
):
    share, hidden = weight_hbm.shape
    stores = []
    for i in range(share // chunk):
        here = slice(i * chunk, (i + 1) * chunk)
        weight_buf[here, :] = lax.dot_general(
            arrived_ref[:, here], scaled_ref[...], (((0,), (0,)), ((), ())), preferred_element_type=F32
        ).astype(BF16)
        stores.append(pltpu.make_async_copy(weight_buf.at[here, :], weight_hbm.at[here, :], weight_sems.at[i]))
        stores[-1].start()
    for d in range(n_data):
        total = sum(
            lax.dot_general(hits_ref[d, i], arrived_ref[...], (((0,), (0,)), ((), ())), preferred_element_type=F32)
            for i in range(2)
        )
        token_buf[:, d * share : (d + 1) * share] = total.astype(BF16)
    stores.append(pltpu.make_async_copy(token_buf, token_hbm, token_sem))
    stores[-1].start()
    for store in stores:
        store.wait()


def local(tokens, proj_weight, slot_grads, gate_weights, selected):
    n_tensor = lax.axis_size("tensor")
    n_expert = lax.axis_size("expert")
    n_data = lax.axis_size("dp")
    order = exchange_order(n_expert, n_tensor, n_data)
    members = len(order)
    tok_dev, features = tokens.shape[1:]
    hidden = proj_weight.shape[2]
    experts, capacity = selected.shape[1:]
    share = features // n_data
    chosen, gate, grads = selected[0], gate_weights[0], slot_grads[0, 0]
    swap = [(0, 1), (1, 0)]
    other_grads = lax.ppermute(grads, "dp", swap)
    other_chosen = lax.ppermute(chosen, "dp", swap)
    rows, own_grads, placed, place, hits = pl.pallas_call(
        functools.partial(prep_kernel, order, n_expert, n_tensor, n_data),
        out_shape=(
            jax.ShapeDtypeStruct((members * BLOCK, share), BF16),
            jax.ShapeDtypeStruct((capacity, hidden), BF16),
            jax.ShapeDtypeStruct((members * BLOCK, hidden), BF16),
            jax.ShapeDtypeStruct((1, capacity), jnp.int32),
            jax.ShapeDtypeStruct((n_data, 2, members * BLOCK, tok_dev), BF16),
        ),
        in_specs=[HBM] * 4,
        out_specs=(VMEM,) * 5,
        scratch_shapes=[
            pltpu.VMEM((experts, capacity), jnp.int32),
            pltpu.VMEM((experts, capacity), F32),
            pltpu.VMEM((tok_dev, features), BF16),
            DMA((4,)),
        ],
        compiler_params=params(),
        cost_estimate=cost(12 * 10**8, 10**6),
        name="prep",
    )(*(pltpu.with_memory_space_constraint(x, pltpu.HBM) for x in (chosen, gate, grads, tokens[0])))
    send, scaled_all = pl.pallas_call(
        functools.partial(partial_kernel, order, n_expert, n_tensor, tok_dev),
        out_shape=(
            jax.ShapeDtypeStruct((members * BLOCK, share), BF16),
            jax.ShapeDtypeStruct((members * BLOCK, hidden), BF16),
        ),
        in_specs=[VMEM] * 7,
        out_specs=(VMEM, VMEM),
        compiler_params=params(),
        cost_estimate=cost(10**9, 4 * 10**6),
        name="partial",
    )(other_chosen, other_grads, proj_weight[0], rows, own_grads, placed, place)
    arrived = lax.all_to_all(
        send.reshape(members, BLOCK, share),
        ("expert", "dp", "tensor"),
        split_axis=0,
        concat_axis=0,
        tiled=True,
        axis_index_groups=[[(h * n_data + d) * n_tensor + t for d, h, t in order]],
    )
    chunk = min(128, share)
    weight_grads, token_grads = pl.pallas_call(
        functools.partial(finish_kernel, n_data, chunk),
        out_shape=(
            jax.ShapeDtypeStruct((share, hidden), BF16),
            jax.ShapeDtypeStruct((tok_dev, features), BF16),
        ),
        in_specs=[VMEM] * 3,
        out_specs=(HBM, HBM),
        scratch_shapes=[
            pltpu.VMEM((share, hidden), BF16),
            pltpu.VMEM((tok_dev, features), BF16),
            DMA((share // chunk,)),
            DMA,
        ],
        compiler_params=params(),
        cost_estimate=cost(10**9, 4 * 10**6),
        name="finish",
    )(arrived.reshape(members * BLOCK, share), scaled_all, hits)
    return token_grads[None], weight_grads[None]


def solution(mesh):
    in_specs = (
        P("dp", ("groups", "expert", "tensor"), None),
        P("expert", "dp", "tensor"),
        P("dp", "expert", "groups", "tensor"),
        P("dp", None, "groups"),
        P("dp", None, "groups"),
    )
    out_specs = (
        P("dp", ("groups", "expert", "tensor"), None),
        P(("groups", "expert"), "dp", "tensor"),
    )
    return jax.shard_map(local, mesh=mesh, in_specs=in_specs, out_specs=out_specs, check_vma=False)
```

time: 24.5 us -> 20.6 us (0.84)
  the two profiles are of different devices: /device:TPU:0 before, /device:TPU:1 now
where the time goes in v4:
time: 20.6 us; the launch traced here: 20.4 us
  blocking collectives  13.4 us (65%)
  Pallas kernels  5.7 us (28%)
  between operations  0.68 us (3%)
  starting transfers between devices  0.58 us (3%)
    all_to_all x1, blocking collectives, local(): lax.all_to_all(send.reshape(members, BLOCK, share), ('expert', 'dp', 'ten...  13.4 us
    pallas_call x1, Pallas kernels, local(): pl.pallas_call(functools.partial(finish_kernel, n_data, chunk), out_shape...  2.4 us
    pallas_call x1, Pallas kernels, local(): pl.pallas_call(functools.partial(prep_kernel, order, n_expert, n_tensor,...  1.76 us
    pallas_call x1, Pallas kernels, local(): pl.pallas_call(functools.partial(partial_kernel, order, n_expert, n_tenso...  1.54 us
    ppermute x1, starting transfers between devices, local(): other_grads = lax.ppermute(grads, 'dp', swap)  0.49 us
  transfers between devices with their start and end apart: 2, of which 0 were waited for; matrix products, arithmetic and copies ran while one was open for 0% of the time, Pallas kernels for 9%

profile of v4, /device:TPU:1, one launch (start us, length us, event | category | flops | bytes accessed | tf_op | source)
XLA Modules:
  0.0 20.4 jit_solution(5496061859267410413)
XLA Ops:
  0.6 0.0 copy-start
  0.6 0.1 collective-permute-start
  0.7 0.5 %collective-permute-start.1 = (bf16[16,1792]{1,0:T(8,128)(2,1)}, bf16[16,1792]{1,0:T(8,128)(2,1)S(1)}, u32[]{:S(2)}, u32[]{:S(2)}) collective-permute-start(bf16[16,1792]{1,0:T(8,128)(2,1)} %bitcast.13), channel_id=1, source_target_pairs={{0,2},{2,0},{1,3},{3,1},{4,6},{6,4},{5,7},{7,5},{8,10},{10,8},{9,1... | collective-permute-start | bytes 172040 | tf_op jit(solution)/shard_map/ppermute | solution.py:221
  1.2 1.8 %prep.1 = (bf16[128,1024]{1,0:T(8,128)(2,1)S(1)}, bf16[16,1792]{1,0:T(8,128)(2,1)S(1)}, bf16[128,1792]{1,0:T(8,128)(2,1)S(1)}, s32[1,16]{1,0:T(1,128)S(1)}, bf16[2,2,128,128]{3,2,1,0:T(8,128)(2,1)S(1)}) custom-call(s32[2,16]{1,0:T(2,128)} %bitcast.17, f32[2,16]{1,0:T(2,128)} %bitcast.15, bf16[16,1792]{1,0:T(8,128)(2,1)} %bitcast.14, bf16[128,2048]{1,0:T(8,128)(2,1)} %bitcast.12), custom_call_target="tpu_custom_call" | custom-call | flops 1200000000 | bytes 1000000 | tf_op jit(solution)/shard_map/prep/pallas_call | solution.py:223
  3.0 0.0 collective-permute-done.chosen_ref
  3.0 0.0 collective-permute-done.1.other_ref
  3.0 0.0 copy-done
  3.0 1.5 %partial.1 = (bf16[128,1024]{1,0:T(8,128)(2,1)S(1)}, bf16[128,1792]{1,0:T(8,128)(2,1)S(1)}) custom-call(s32[2,16]{1,0:T(2,128)S(1)} %collective-permute-done.chosen_ref, bf16[16,1792]{1,0:T(8,128)(2,1)S(1)} %collective-permute-done.1.other_ref, bf16[1024,1792]{1,0:T(8,128)(2,1)S(1)} %bitcast.9, bf16[128,1024]{1,0:T(8,128)(2,1)S(1)} %get-tuple-element.11.rows_ref, ...), custom_call_target="tpu_custom_call" | custom-call | flops 1000000000 | bytes 4000000 | tf_op jit(solution)/shard_map/partial/pallas_call | solution.py:244
  4.6 13.4 %all_to_all.5 = bf16[16,8,1024]{2,1,0:T(8,128)(2,1)S(1)} all-to-all(bf16[16,8,1024]{2,1,0:T(8,128)(2,1)S(1)} %bitcast.10), channel_id=1, replica_groups={{11,12,6,9,3,4,15,1,10,13,7,8,2,5,14,0},{27,28,22,25,19,20,31,17,26,29,..., dimensions={0} | all-to-all | bytes 524288 | tf_op jit(solution)/shard_map/all_to_all | solution.py:256
  18.0 2.4 %finish.1 = (bf16[1024,1792]{1,0:T(8,128)(2,1)}, bf16[128,2048]{1,0:T(8,128)(2,1)}) custom-call(bf16[128,1024]{1,0:T(8,128)(2,1)S(1)} %bitcast.11, bf16[128,1792]{1,0:T(8,128)(2,1)S(1)} %get-tuple-element.16.scaled_ref, bf16[2,2,128,128]{3,2,1,0:T(8,128)(2,1)S(1)} %get-tuple-element.17.hits_ref), custom_call_target="tpu_custom_call" | custom-call | flops 1000000000 | bytes 4000000 | tf_op jit(solution)/shard_map/finish/pallas_call | solution.py:265
Async XLA Ops:
  0.6 2.4 %copy-start = (bf16[1,1024,1792]{2,1,0:T(8,128)(2,1)S(1)}, bf16[1,1024,1792]{2,1,0:T(8,128)(2,1)}, u32[]{:S(2)}) copy-start(bf16[1,1024,1792]{2,1,0:T(8,128)(2,1)} %param.6) | copy-start | bytes 11010052
  0.6 2.4 %collective-permute-start = (s32[2,16]{1,0:T(2,128)}, s32[2,16]{1,0:T(2,128)S(1)}, u32[]{:S(2)}, u32[]{:S(2)}) collective-permute-start(s32[2,16]{1,0:T(2,128)} %bitcast.16), channel_id=1, source_target_pairs={{0,2},{2,0},{1,3},{3,1},{4,6},{6,4},{5,7},{7,5},{8,10},{10,8},{9,1... | collective-permute-start | bytes 392 | tf_op jit(solution)/shard_map/ppermute | solution.py:222
  0.7 2.3 %collective-permute-start.1 = (bf16[16,1792]{1,0:T(8,128)(2,1)}, bf16[16,1792]{1,0:T(8,128)(2,1)S(1)}, u32[]{:S(2)}, u32[]{:S(2)}) collective-permute-start(bf16[16,1792]{1,0:T(8,128)(2,1)} %bitcast.13), channel_id=1, source_target_pairs={{0,2},{2,0},{1,3},{3,1},{4,6},{6,4},{5,7},{7,5},{8,10},{10,8},{9,1... | collective-permute-start | bytes 172040 | tf_op jit(solution)/shard_map/ppermute | solution.py:221

commit v5 on v4

--- a/solution.py
+++ b/solution.py
@@ -12,6 +12,8 @@
 BLOCK = 2 * MOST
 STRIDE = 11
 START = 12
+EARLIER = 3
+LATER = 7
 BF16 = jnp.bfloat16
 F32 = jnp.float32
 VMEM = pl.BlockSpec(memory_space=pltpu.VMEM)
@@ -33,7 +35,9 @@
     ]
     n = len(walk)
     stride = STRIDE if math.gcd(STRIDE, n) == 1 else 1
-    return [walk[(stride * k + START) % n] for k in range(n)]
+    order = [walk[(stride * k + START) % n] for k in range(n)]
+    order.insert(LATER % n, order.pop(EARLIER % n))
+    return order
 
 
 def to_column(row):
@@ -88,7 +92,6 @@
     tokens_hbm,
     send_ref,
     grads_ref,
-    placed_ref,
     place_ref,
     hits_ref,
     chosen_ref,
@@ -135,8 +138,6 @@
     rows = lax.broadcasted_iota(jnp.int32, (experts * BLOCK, tok_dev), 1) + 1
     pick = as_onehot(rows == jnp.concatenate([p for target in targets for p in (target, none)], axis=0))
     gate = jnp.concatenate([p for g in gates for p in (g, no_gate)], axis=0)
-    loads[2].wait()
-    placed_ref[...] = jnp.dot(spread(place, blocks), grads_ref[...], preferred_element_type=F32).astype(BF16)
     loads[3].wait()
     picked = gate * jnp.dot(pick, tokens_ref[...], preferred_element_type=F32)
     for k, (d, h, t) in enumerate(order):
@@ -144,6 +145,7 @@
         send_ref[k * BLOCK : (k + 1) * BLOCK, :] = picked[
             e * BLOCK : (e + 1) * BLOCK, d * share : (d + 1) * share
         ].astype(BF16)
+    loads[2].wait()
 
 
 def partial_kernel(
@@ -156,30 +158,23 @@
     weight_ref,
     rows_ref,
     grads_ref,
-    placed_ref,
     place_ref,
     send_ref,
     all_ref,
 ):
     blocks = len(order)
     halves = n_expert // chosen_ref.shape[0]
-    capacity = chosen_ref.shape[1]
     own_expert = lax.axis_index("expert") // halves
     owner, arrival = owner_and_arrival(chosen_ref[pl.ds(own_expert, 1), :], tok_dev)
-    place = block_of(order, owner, 1 - lax.axis_index("dp"), n_tensor) * BLOCK + arrival
-    other = other_ref[...]
+    other = block_of(order, owner, 1 - lax.axis_index("dp"), n_tensor) * BLOCK + arrival
+    place = jnp.concatenate([place_ref[...], other], axis=1)
+    grads = jnp.concatenate([grads_ref[...], other_ref[...]], axis=0)
+    all_ref[...] = jnp.dot(spread(place, blocks), grads, preferred_element_type=F32).astype(BF16)
     part = lax.dot_general(
-        jnp.concatenate([grads_ref[...], other], axis=0),
-        weight_ref[...],
-        (((1,), (1,)), ((), ())),
-        preferred_element_type=F32,
+        grads, weight_ref[...], (((1,), (1,)), ((), ())), preferred_element_type=F32
     ).astype(BF16)
-    out = rows_ref[...].astype(F32)
-    for put, piece in ((place_ref[...], part[:capacity]), (place, part[capacity:])):
-        out = out + jnp.dot(spread(put + MOST, blocks), piece, preferred_element_type=F32)
-    send_ref[...] = out.astype(BF16)
-    theirs = jnp.dot(spread(place, blocks), other, preferred_element_type=F32)
-    all_ref[...] = (placed_ref[...].astype(F32) + theirs).astype(BF16)
+    out = jnp.dot(spread(place + MOST, blocks), part, preferred_element_type=F32)
+    send_ref[...] = (out + rows_ref[...].astype(F32)).astype(BF16)
 
 
 def finish_kernel(
@@ -220,17 +215,16 @@
     swap = [(0, 1), (1, 0)]
     other_grads = lax.ppermute(grads, "dp", swap)
     other_chosen = lax.ppermute(chosen, "dp", swap)
-    rows, own_grads, placed, place, hits = pl.pallas_call(
+    rows, own_grads, place, hits = pl.pallas_call(
         functools.partial(prep_kernel, order, n_expert, n_tensor, n_data),
         out_shape=(
             jax.ShapeDtypeStruct((members * BLOCK, share), BF16),
             jax.ShapeDtypeStruct((capacity, hidden), BF16),
-            jax.ShapeDtypeStruct((members * BLOCK, hidden), BF16),
             jax.ShapeDtypeStruct((1, capacity), jnp.int32),
             jax.ShapeDtypeStruct((n_data, 2, members * BLOCK, tok_dev), BF16),
         ),
         in_specs=[HBM] * 4,
-        out_specs=(VMEM,) * 5,
+        out_specs=(VMEM,) * 4,
         scratch_shapes=[
             pltpu.VMEM((experts, capacity), jnp.int32),
             pltpu.VMEM((experts, capacity), F32),
@@ -247,12 +241,12 @@
             jax.ShapeDtypeStruct((members * BLOCK, share), BF16),
             jax.ShapeDtypeStruct((members * BLOCK, hidden), BF16),
         ),
-        in_specs=[VMEM] * 7,
+        in_specs=[VMEM] * 6,
         out_specs=(VMEM, VMEM),
         compiler_params=params(),
         cost_estimate=cost(10**9, 4 * 10**6),
         name="partial",
-    )(other_chosen, other_grads, proj_weight[0], rows, own_grads, placed, place)
+    )(other_chosen, other_grads, proj_weight[0], rows, own_grads, place)
     arrived = lax.all_to_all(
         send.reshape(members, BLOCK, share),
         ("expert", "dp", "tensor"),

time: 20.6 us -> 20.3 us (0.985)
  transfers between devices with their start and end apart: 2 -> 2, of which waited for: 0 -> 0; matrix products, arithmetic and copies ran while one was open for 0% -> 0% of each run, Pallas kernels for 9% -> 8%
where the time goes in v5:
time: 20.3 us; the launch traced here: 20.1 us
  blocking collectives  13.2 us (65%)
  Pallas kernels  5.6 us (28%)
  between operations  0.67 us (3%)
  starting transfers between devices  0.58 us (3%)
    all_to_all x1, blocking collectives, local(): lax.all_to_all(send.reshape(members, BLOCK, share), ('expert', 'dp', 'ten...  13.2 us
    pallas_call x1, Pallas kernels, local(): pl.pallas_call(functools.partial(finish_kernel, n_data, chunk), out_shape...  2.4 us
    pallas_call x1, Pallas kernels, local(): pl.pallas_call(functools.partial(prep_kernel, order, n_expert, n_tensor,...  1.61 us
    pallas_call x1, Pallas kernels, local(): pl.pallas_call(functools.partial(partial_kernel, order, n_expert, n_tenso...  1.59 us
    ppermute x1, starting transfers between devices, local(): other_grads = lax.ppermute(grads, 'dp', swap)  0.49 us
  transfers between devices with their start and end apart: 2, of which 0 were waited for; matrix products, arithmetic and copies ran while one was open for 0% of the time, Pallas kernels for 8%

profile of v5, /device:TPU:1, one launch (start us, length us, event | category | flops | bytes accessed | tf_op | source)
XLA Modules:
  0.0 20.1 jit_solution(2518302299421331459)
XLA Ops:
  0.6 0.0 copy-start
  0.6 0.1 collective-permute-start
  0.7 0.5 %collective-permute-start.1 = (bf16[16,1792]{1,0:T(8,128)(2,1)}, bf16[16,1792]{1,0:T(8,128)(2,1)S(1)}, u32[]{:S(2)}, u32[]{:S(2)}) collective-permute-start(bf16[16,1792]{1,0:T(8,128)(2,1)} %bitcast.13), channel_id=1, source_target_pairs={{0,2},{2,0},{1,3},{3,1},{4,6},{6,4},{5,7},{7,5},{8,10},{10,8},{9,1... | collective-permute-start | bytes 172040 | tf_op jit(solution)/shard_map/ppermute | solution.py:216
  1.2 1.6 %prep.1 = (bf16[128,1024]{1,0:T(8,128)(2,1)S(1)}, bf16[16,1792]{1,0:T(8,128)(2,1)S(1)}, s32[1,16]{1,0:T(1,128)S(1)}, bf16[2,2,128,128]{3,2,1,0:T(8,128)(2,1)S(1)}) custom-call(s32[2,16]{1,0:T(2,128)} %bitcast.17, f32[2,16]{1,0:T(2,128)} %bitcast.15, bf16[16,1792]{1,0:T(8,128)(2,1)} %bitcast.14, bf16[128,2048]{1,0:T(8,128)(2,1)} %bitcast.12), custom_call_target="tpu_custom_call" | custom-call | flops 1200000000 | bytes 1000000 | tf_op jit(solution)/shard_map/prep/pallas_call | solution.py:218
  2.8 0.0 collective-permute-done.chosen_ref
  2.8 0.0 collective-permute-done.1.other_ref
  2.9 0.0 copy-done
  2.9 1.6 %partial.1 = (bf16[128,1024]{1,0:T(8,128)(2,1)S(1)}, bf16[128,1792]{1,0:T(8,128)(2,1)S(1)}) custom-call(s32[2,16]{1,0:T(2,128)S(1)} %collective-permute-done.chosen_ref, bf16[16,1792]{1,0:T(8,128)(2,1)S(1)} %collective-permute-done.1.other_ref, bf16[1024,1792]{1,0:T(8,128)(2,1)S(1)} %bitcast.9, bf16[128,1024]{1,0:T(8,128)(2,1)S(1)} %get-tuple-element.10.rows_ref, ...), custom_call_target="tpu_custom_call" | custom-call | flops 1000000000 | bytes 4000000 | tf_op jit(solution)/shard_map/partial/pallas_call | solution.py:238
  4.5 13.2 %all_to_all.5 = bf16[16,8,1024]{2,1,0:T(8,128)(2,1)S(1)} all-to-all(bf16[16,8,1024]{2,1,0:T(8,128)(2,1)S(1)} %bitcast.10), channel_id=1, replica_groups={{11,12,6,3,4,15,1,9,10,13,7,8,2,5,14,0},{27,28,22,19,20,31,17,25,26,29,..., dimensions={0} | all-to-all | bytes 524288 | tf_op jit(solution)/shard_map/all_to_all | solution.py:250
  17.7 2.4 %finish.1 = (bf16[1024,1792]{1,0:T(8,128)(2,1)}, bf16[128,2048]{1,0:T(8,128)(2,1)}) custom-call(bf16[128,1024]{1,0:T(8,128)(2,1)S(1)} %bitcast.11, bf16[128,1792]{1,0:T(8,128)(2,1)S(1)} %get-tuple-element.14.scaled_ref, bf16[2,2,128,128]{3,2,1,0:T(8,128)(2,1)S(1)} %get-tuple-element.15.hits_ref), custom_call_target="tpu_custom_call" | custom-call | flops 1000000000 | bytes 4000000 | tf_op jit(solution)/shard_map/finish/pallas_call | solution.py:259
Async XLA Ops:
  0.6 2.3 %copy-start = (bf16[1,1024,1792]{2,1,0:T(8,128)(2,1)S(1)}, bf16[1,1024,1792]{2,1,0:T(8,128)(2,1)}, u32[]{:S(2)}) copy-start(bf16[1,1024,1792]{2,1,0:T(8,128)(2,1)} %param.6) | copy-start | bytes 11010052
  0.6 2.2 %collective-permute-start = (s32[2,16]{1,0:T(2,128)}, s32[2,16]{1,0:T(2,128)S(1)}, u32[]{:S(2)}, u32[]{:S(2)}) collective-permute-start(s32[2,16]{1,0:T(2,128)} %bitcast.16), channel_id=1, source_target_pairs={{0,2},{2,0},{1,3},{3,1},{4,6},{6,4},{5,7},{7,5},{8,10},{10,8},{9,1... | collective-permute-start | bytes 392 | tf_op jit(solution)/shard_map/ppermute | solution.py:217
  0.7 2.1 %collective-permute-start.1 = (bf16[16,1792]{1,0:T(8,128)(2,1)}, bf16[16,1792]{1,0:T(8,128)(2,1)S(1)}, u32[]{:S(2)}, u32[]{:S(2)}) collective-permute-start(bf16[16,1792]{1,0:T(8,128)(2,1)} %bitcast.13), channel_id=1, source_target_pairs={{0,2},{2,0},{1,3},{3,1},{4,6},{6,4},{5,7},{7,5},{8,10},{10,8},{9,1... | collective-permute-start | bytes 172040 | tf_op jit(solution)/shard_map/ppermute | solution.py:216

commit v6 on v5

--- a/solution.py
+++ b/solution.py
@@ -169,12 +169,12 @@
     other = block_of(order, owner, 1 - lax.axis_index("dp"), n_tensor) * BLOCK + arrival
     place = jnp.concatenate([place_ref[...], other], axis=1)
     grads = jnp.concatenate([grads_ref[...], other_ref[...]], axis=0)
-    all_ref[...] = jnp.dot(spread(place, blocks), grads, preferred_element_type=F32).astype(BF16)
     part = lax.dot_general(
         grads, weight_ref[...], (((1,), (1,)), ((), ())), preferred_element_type=F32
     ).astype(BF16)
     out = jnp.dot(spread(place + MOST, blocks), part, preferred_element_type=F32)
     send_ref[...] = (out + rows_ref[...].astype(F32)).astype(BF16)
+    all_ref[...] = jnp.dot(spread(place, blocks), grads, preferred_element_type=F32).astype(BF16)
 
 
 def finish_kernel(

time: 20.3 us -> 20.2 us (level)
  no operation moved by 1% of the time
where the time goes in v6:
time: 20.2 us; the launch traced here: 20 us
  blocking collectives  13.2 us (65%)
  Pallas kernels  5.49 us (27%)
  between operations  0.67 us (3%)
  starting transfers between devices  0.58 us (3%)
    all_to_all x1, blocking collectives, local(): lax.all_to_all(send.reshape(members, BLOCK, share), ('expert', 'dp', 'ten...  13.2 us
    pallas_call x1, Pallas kernels, local(): pl.pallas_call(functools.partial(finish_kernel, n_data, chunk), out_shape...  2.4 us
    pallas_call x1, Pallas kernels, local(): pl.pallas_call(functools.partial(prep_kernel, order, n_expert, n_tensor,...  1.61 us
    pallas_call x1, Pallas kernels, local(): pl.pallas_call(functools.partial(partial_kernel, order, n_expert, n_tenso...  1.48 us
    ppermute x1, starting transfers between devices, local(): other_grads = lax.ppermute(grads, 'dp', swap)  0.49 us
  transfers between devices with their start and end apart: 2, of which 0 were waited for; matrix products, arithmetic and copies ran while one was open for 0% of the time, Pallas kernels for 8%

profile of v6, /device:TPU:1, one launch (start us, length us, event | category | flops | bytes accessed | tf_op | source)
XLA Modules:
  0.0 20.0 jit_solution(4165309960325515323)
XLA Ops:
  0.6 0.0 copy-start
  0.6 0.1 collective-permute-start
  0.7 0.5 %collective-permute-start.1 = (bf16[16,1792]{1,0:T(8,128)(2,1)}, bf16[16,1792]{1,0:T(8,128)(2,1)S(1)}, u32[]{:S(2)}, u32[]{:S(2)}) collective-permute-start(bf16[16,1792]{1,0:T(8,128)(2,1)} %bitcast.13), channel_id=1, source_target_pairs={{0,2},{2,0},{1,3},{3,1},{4,6},{6,4},{5,7},{7,5},{8,10},{10,8},{9,1... | collective-permute-start | bytes 172040 | tf_op jit(solution)/shard_map/ppermute | solution.py:216
  1.2 1.6 %prep.1 = (bf16[128,1024]{1,0:T(8,128)(2,1)S(1)}, bf16[16,1792]{1,0:T(8,128)(2,1)S(1)}, s32[1,16]{1,0:T(1,128)S(1)}, bf16[2,2,128,128]{3,2,1,0:T(8,128)(2,1)S(1)}) custom-call(s32[2,16]{1,0:T(2,128)} %bitcast.17, f32[2,16]{1,0:T(2,128)} %bitcast.15, bf16[16,1792]{1,0:T(8,128)(2,1)} %bitcast.14, bf16[128,2048]{1,0:T(8,128)(2,1)} %bitcast.12), custom_call_target="tpu_custom_call" | custom-call | flops 1200000000 | bytes 1000000 | tf_op jit(solution)/shard_map/prep/pallas_call | solution.py:218
  2.8 0.0 collective-permute-done.chosen_ref
  2.8 0.0 collective-permute-done.1.other_ref
  2.9 0.0 copy-done
  2.9 1.5 %partial.1 = (bf16[128,1024]{1,0:T(8,128)(2,1)S(1)}, bf16[128,1792]{1,0:T(8,128)(2,1)S(1)}) custom-call(s32[2,16]{1,0:T(2,128)S(1)} %collective-permute-done.chosen_ref, bf16[16,1792]{1,0:T(8,128)(2,1)S(1)} %collective-permute-done.1.other_ref, bf16[1024,1792]{1,0:T(8,128)(2,1)S(1)} %bitcast.9, bf16[128,1024]{1,0:T(8,128)(2,1)S(1)} %get-tuple-element.10.rows_ref, ...), custom_call_target="tpu_custom_call" | custom-call | flops 1000000000 | bytes 4000000 | tf_op jit(solution)/shard_map/partial/pallas_call | solution.py:238
  4.4 13.2 %all_to_all.5 = bf16[16,8,1024]{2,1,0:T(8,128)(2,1)S(1)} all-to-all(bf16[16,8,1024]{2,1,0:T(8,128)(2,1)S(1)} %bitcast.10), channel_id=1, replica_groups={{11,12,6,3,4,15,1,9,10,13,7,8,2,5,14,0},{27,28,22,19,20,31,17,25,26,29,..., dimensions={0} | all-to-all | bytes 524288 | tf_op jit(solution)/shard_map/all_to_all | solution.py:250
  17.6 2.4 %finish.1 = (bf16[1024,1792]{1,0:T(8,128)(2,1)}, bf16[128,2048]{1,0:T(8,128)(2,1)}) custom-call(bf16[128,1024]{1,0:T(8,128)(2,1)S(1)} %bitcast.11, bf16[128,1792]{1,0:T(8,128)(2,1)S(1)} %get-tuple-element.14.scaled_ref, bf16[2,2,128,128]{3,2,1,0:T(8,128)(2,1)S(1)} %get-tuple-element.15.hits_ref), custom_call_target="tpu_custom_call" | custom-call | flops 1000000000 | bytes 4000000 | tf_op jit(solution)/shard_map/finish/pallas_call | solution.py:259
Async XLA Ops:
  0.6 2.3 %copy-start = (bf16[1,1024,1792]{2,1,0:T(8,128)(2,1)S(1)}, bf16[1,1024,1792]{2,1,0:T(8,128)(2,1)}, u32[]{:S(2)}) copy-start(bf16[1,1024,1792]{2,1,0:T(8,128)(2,1)} %param.6) | copy-start | bytes 11010052
  0.6 2.2 %collective-permute-start = (s32[2,16]{1,0:T(2,128)}, s32[2,16]{1,0:T(2,128)S(1)}, u32[]{:S(2)}, u32[]{:S(2)}) collective-permute-start(s32[2,16]{1,0:T(2,128)} %bitcast.16), channel_id=1, source_target_pairs={{0,2},{2,0},{1,3},{3,1},{4,6},{6,4},{5,7},{7,5},{8,10},{10,8},{9,1... | collective-permute-start | bytes 392 | tf_op jit(solution)/shard_map/ppermute | solution.py:217
  0.7 2.1 %collective-permute-start.1 = (bf16[16,1792]{1,0:T(8,128)(2,1)}, bf16[16,1792]{1,0:T(8,128)(2,1)S(1)}, u32[]{:S(2)}, u32[]{:S(2)}) collective-permute-start(bf16[16,1792]{1,0:T(8,128)(2,1)} %bitcast.13), channel_id=1, source_target_pairs={{0,2},{2,0},{1,3},{3,1},{4,6},{6,4},{5,7},{7,5},{8,10},{10,8},{9,1... | collective-permute-start | bytes 172040 | tf_op jit(solution)/shard_map/ppermute | solution.py:216

commit v7 on v6

--- a/solution.py
+++ b/solution.py
@@ -14,6 +14,7 @@
 START = 12
 EARLIER = 3
 LATER = 7
+EXCHANGED = ((6, 10), (8, 14))
 BF16 = jnp.bfloat16
 F32 = jnp.float32
 VMEM = pl.BlockSpec(memory_space=pltpu.VMEM)
@@ -37,6 +38,8 @@
     stride = STRIDE if math.gcd(STRIDE, n) == 1 else 1
     order = [walk[(stride * k + START) % n] for k in range(n)]
     order.insert(LATER % n, order.pop(EARLIER % n))
+    for i, j in EXCHANGED:
+        order[i % n], order[j % n] = order[j % n], order[i % n]
     return order
 
 
@@ -126,15 +129,6 @@
     place_ref[...] = place
     targets, gates = own_places(chosen_ref, gate_ref, slots, owner_id, tok_dev)
     none, no_gate = jnp.zeros_like(targets[0]), jnp.zeros_like(gates[0])
-    rows = lax.broadcasted_iota(jnp.int32, (blocks * BLOCK, tok_dev), 1) + 1
-    for side in range(n_data):
-        ours = [h // halves if d == side else None for d, h, t in order]
-        target = jnp.concatenate([p for e in ours for p in (none, none if e is None else targets[e])], axis=0)
-        gate = jnp.concatenate([p for e in ours for p in (no_gate, no_gate if e is None else gates[e])], axis=0)
-        weighted = jnp.where(rows == target, gate, 0.0)
-        high = weighted.astype(BF16)
-        hits_ref[side, 0] = high
-        hits_ref[side, 1] = (weighted - high.astype(F32)).astype(BF16)
     rows = lax.broadcasted_iota(jnp.int32, (experts * BLOCK, tok_dev), 1) + 1
     pick = as_onehot(rows == jnp.concatenate([p for target in targets for p in (target, none)], axis=0))
     gate = jnp.concatenate([p for g in gates for p in (g, no_gate)], axis=0)
@@ -145,6 +139,15 @@
         send_ref[k * BLOCK : (k + 1) * BLOCK, :] = picked[
             e * BLOCK : (e + 1) * BLOCK, d * share : (d + 1) * share
         ].astype(BF16)
+    rows = lax.broadcasted_iota(jnp.int32, (blocks * BLOCK, tok_dev), 1) + 1
+    for side in range(n_data):
+        ours = [h // halves if d == side else None for d, h, t in order]
+        target = jnp.concatenate([p for e in ours for p in (none, none if e is None else targets[e])], axis=0)
+        gate = jnp.concatenate([p for e in ours for p in (no_gate, no_gate if e is None else gates[e])], axis=0)
+        weighted = jnp.where(rows == target, gate, 0.0)
+        high = weighted.astype(BF16)
+        hits_ref[side, 0] = high
+        hits_ref[side, 1] = (weighted - high.astype(F32)).astype(BF16)
     loads[2].wait()
 
 

time: 20.2 us -> 20.1 us (level)
  the two profiles are of different devices: /device:TPU:1 before, /device:TPU:0 now
where the time goes in v7:
time: 20.1 us; the launch traced here: 19.9 us
  blocking collectives  13.1 us (65%)
  Pallas kernels  5.53 us (28%)
  between operations  0.68 us (3%)
  starting transfers between devices  0.64 us (3%)
    all_to_all x1, blocking collectives, local(): lax.all_to_all(send.reshape(members, BLOCK, share), ('expert', 'dp', 'ten...  13.1 us
    pallas_call x1, Pallas kernels, local(): pl.pallas_call(functools.partial(finish_kernel, n_data, chunk), out_shape...  2.4 us
    pallas_call x1, Pallas kernels, local(): pl.pallas_call(functools.partial(prep_kernel, order, n_expert, n_tensor,...  1.65 us
    pallas_call x1, Pallas kernels, local(): pl.pallas_call(functools.partial(partial_kernel, order, n_expert, n_tenso...  1.49 us
    ppermute x1, starting transfers between devices, local(): other_chosen = lax.ppermute(chosen, 'dp', swap)  0.56 us
  transfers between devices with their start and end apart: 2, of which 0 were waited for; matrix products, arithmetic and copies ran while one was open for 0% of the time, Pallas kernels for 8%

profile of v7, /device:TPU:0, one launch (start us, length us, event | category | flops | bytes accessed | tf_op | source)
XLA Modules:
  0.0 19.9 jit_solution(4293998691752937782)
XLA Ops:
  0.6 0.0 copy-start
  0.6 0.6 %collective-permute-start = (s32[2,16]{1,0:T(2,128)}, s32[2,16]{1,0:T(2,128)S(1)}, u32[]{:S(2)}, u32[]{:S(2)}) collective-permute-start(s32[2,16]{1,0:T(2,128)} %bitcast.16), channel_id=1, source_target_pairs={{0,2},{2,0},{1,3},{3,1},{4,6},{6,4},{5,7},{7,5},{8,10},{10,8},{9,1... | collective-permute-start | bytes 392 | tf_op jit(solution)/shard_map/ppermute | solution.py:220
  1.2 0.1 collective-permute-start.1
  1.3 1.6 %prep.1 = (bf16[128,1024]{1,0:T(8,128)(2,1)S(1)}, bf16[16,1792]{1,0:T(8,128)(2,1)S(1)}, s32[1,16]{1,0:T(1,128)S(1)}, bf16[2,2,128,128]{3,2,1,0:T(8,128)(2,1)S(1)}) custom-call(s32[2,16]{1,0:T(2,128)} %bitcast.17, f32[2,16]{1,0:T(2,128)} %bitcast.15, bf16[16,1792]{1,0:T(8,128)(2,1)} %bitcast.14, bf16[128,2048]{1,0:T(8,128)(2,1)} %bitcast.12), custom_call_target="tpu_custom_call" | custom-call | flops 1200000000 | bytes 1000000 | tf_op jit(solution)/shard_map/prep/pallas_call | solution.py:221
  2.9 0.0 collective-permute-done.chosen_ref
  2.9 0.0 collective-permute-done.1.other_ref
  3.0 0.0 copy-done
  3.0 1.5 %partial.1 = (bf16[128,1024]{1,0:T(8,128)(2,1)S(1)}, bf16[128,1792]{1,0:T(8,128)(2,1)S(1)}) custom-call(s32[2,16]{1,0:T(2,128)S(1)} %collective-permute-done.chosen_ref, bf16[16,1792]{1,0:T(8,128)(2,1)S(1)} %collective-permute-done.1.other_ref, bf16[1024,1792]{1,0:T(8,128)(2,1)S(1)} %bitcast.9, bf16[128,1024]{1,0:T(8,128)(2,1)S(1)} %get-tuple-element.10.rows_ref, ...), custom_call_target="tpu_custom_call" | custom-call | flops 1000000000 | bytes 4000000 | tf_op jit(solution)/shard_map/partial/pallas_call | solution.py:241
  4.5 13.1 %all_to_all.5 = bf16[16,8,1024]{2,1,0:T(8,128)(2,1)S(1)} all-to-all(bf16[16,8,1024]{2,1,0:T(8,128)(2,1)S(1)} %bitcast.10), channel_id=1, replica_groups={{11,12,6,3,4,15,7,9,14,13,1,8,2,5,10,0},{27,28,22,19,20,31,23,25,30,29,..., dimensions={0} | all-to-all | bytes 524288 | tf_op jit(solution)/shard_map/all_to_all | solution.py:253
  17.5 2.4 %finish.1 = (bf16[1024,1792]{1,0:T(8,128)(2,1)}, bf16[128,2048]{1,0:T(8,128)(2,1)}) custom-call(bf16[128,1024]{1,0:T(8,128)(2,1)S(1)} %bitcast.11, bf16[128,1792]{1,0:T(8,128)(2,1)S(1)} %get-tuple-element.14.scaled_ref, bf16[2,2,128,128]{3,2,1,0:T(8,128)(2,1)S(1)} %get-tuple-element.15.hits_ref), custom_call_target="tpu_custom_call" | custom-call | flops 1000000000 | bytes 4000000 | tf_op jit(solution)/shard_map/finish/pallas_call | solution.py:262
Async XLA Ops:
  0.6 2.3 %copy-start = (bf16[1,1024,1792]{2,1,0:T(8,128)(2,1)S(1)}, bf16[1,1024,1792]{2,1,0:T(8,128)(2,1)}, u32[]{:S(2)}) copy-start(bf16[1,1024,1792]{2,1,0:T(8,128)(2,1)} %param.6) | copy-start | bytes 11010052
  0.6 2.3 %collective-permute-start = (s32[2,16]{1,0:T(2,128)}, s32[2,16]{1,0:T(2,128)S(1)}, u32[]{:S(2)}, u32[]{:S(2)}) collective-permute-start(s32[2,16]{1,0:T(2,128)} %bitcast.16), channel_id=1, source_target_pairs={{0,2},{2,0},{1,3},{3,1},{4,6},{6,4},{5,7},{7,5},{8,10},{10,8},{9,1... | collective-permute-start | bytes 392 | tf_op jit(solution)/shard_map/ppermute | solution.py:220
  1.2 1.7 %collective-permute-start.1 = (bf16[16,1792]{1,0:T(8,128)(2,1)}, bf16[16,1792]{1,0:T(8,128)(2,1)S(1)}, u32[]{:S(2)}, u32[]{:S(2)}) collective-permute-start(bf16[16,1792]{1,0:T(8,128)(2,1)} %bitcast.13), channel_id=1, source_target_pairs={{0,2},{2,0},{1,3},{3,1},{4,6},{6,4},{5,7},{7,5},{8,10},{10,8},{9,1... | collective-permute-start | bytes 172040 | tf_op jit(solution)/shard_map/ppermute | solution.py:219
